TPU v7x, 32 devices: a whole 2x2x4 slice. The times are simulated.
32 devices in a mesh: seq: 8 (over z, x), head: 4 (over y, core).
Axes of the slice: x: 2, y: 2, z: 4, core: 2. Of those that a mesh axis runs over, the one named last changes fastest.
Arguments:
- patches: bfloat16 [32768, 768], P('seq'), may hold values from -6 to 6
- slot_image: int32 [128], P('seq'), may hold values from -1 to 63, as said below
- slot_dest: int32 [128], P('seq'), may hold values from -1 to 63, as said below
- enc_gain: float32 [768], replicated, may hold values from 0.1 to 1.9
- w_qkv: bfloat16 [3, 768, 768], P(None, None, 'head'), may hold values from -1.2 to 1.2
- w_out: bfloat16 [768, 768], P('head'), may hold values from -0.21875 to 0.21875
- fast_gain: float32 [768], replicated, may hold values from 0.1 to 1.9
- w_fast: bfloat16 [3, 768, 768], P(None, None, 'head'), may hold values from -0.21875 to 0.21875
- w_rate: bfloat16 [768, 4], P(None, 'head'), may hold values from -0.21875 to 0.21875
- fast_gate_up: float32 [4, 2, 192, 384], P('head'), may hold values from -0.4375 to 0.4375
- fast_down: float32 [4, 384, 192], P('head'), may hold values from -0.3125 to 0.3125
Outputs:
- view_out: bfloat16 [16384, 768], P('seq', 'head')
Inputs may be any that keep to these rules, and one draw needn't show every extreme that they name: slot_dest gives for each slot the view-order block that its block becomes, or -1 for an empty slot; every view-order block is named by exactly one slot. Slots 2i and 2i + 1 of one seq index are both empty or name view blocks 2m and 2m + 1. The slots of one seq index name at most 2 blocks of any one view shard (blocks s * 8 to (s + 1) * 8 - 1), and some seq index uses all of its slots. slot_image is -1 exactly where slot_dest is -1; an image is one block or the two blocks of a slot pair, and different images have different ids.
All inputs are finite; a program needn't handle non-finite values.
Results may differ from a plain program's by a relative error of at most 0.035.
Values may be sent and summed in bfloat16 or wider, within the bound.
A program may use at most 128 MiB of HBM per device.

v0:
```python
import functools

import jax
import jax.numpy as jnp
from jax import lax
from jax.experimental import pallas as pl
from jax.experimental.pallas import tpu as pltpu
from jax.sharding import PartitionSpec as P

HDIM = 64
BLK = 256
BLK_DEV = 8
PAIR = 2 * BLK
EPSILON = 1e-06
RATE_SCALE = 0.1
LANES = 128
MESH = pl.DeviceIdType.MESH
VMEM = pl.BlockSpec(memory_space=pltpu.VMEM)
NT = (((1,), (1,)), ((), ()))


def remote(src, dst, send, recv, device):
    return pltpu.make_async_remote_copy(
        src_ref=src, dst_ref=dst, send_sem=send, recv_sem=recv, device_id=device, device_id_type=MESH
    )


def comm_params(number):
    return pltpu.CompilerParams(
        collective_id=number, has_side_effects=True, vmem_limit_bytes=56 * 1024 * 1024
    )


def greet(devices):
    barrier = pltpu.get_barrier_semaphore()
    for device in devices:
        pl.semaphore_signal(barrier, inc=1, device_id=device, device_id_type=MESH)
    pl.semaphore_wait(barrier, len(devices))


def others(axis_size, me):
    return [lax.rem(me + step, axis_size) for step in range(1, axis_size)]


def head_pals(head_count, head):
    partner = head + 1 - 2 * lax.rem(head, 2)
    peer = lax.rem(head + head_count // 2, head_count)
    return partner, peer


def entry_kernel(n, nh, x_ref, m_ref, w_ref, ox, om, ow, sx, rx, sm, rm, sw, rw):
    seq, head = lax.axis_index("seq"), lax.axis_index("head")
    partner, peer = head_pals(nh, head)
    across = lax.rem(partner + nh // 2, nh)
    targets = others(n, seq)
    greet([(seq, partner), (seq, peer)] + [(to, head) for to in targets])
    to_peer = remote(w_ref, ow.at[:, head], sw.at[0], rw.at[0], (seq, peer))
    to_partner = remote(w_ref, ow.at[:, head], sw.at[1], rw.at[1], (seq, partner))
    to_peer.start()
    to_partner.start()
    copies = []
    for step, to in enumerate(targets):
        copies.append(remote(m_ref.at[to], om.at[seq], sm.at[step], rm.at[step], (to, head)))
        copies.append(remote(x_ref.at[to], ox.at[seq], sx.at[step], rx.at[step], (to, head)))
    for copy in copies:
        copy.start()
    ox[seq] = x_ref[seq]
    om[seq] = m_ref[seq]
    for part in range(w_ref.shape[0]):
        ow[part, head] = w_ref[part]
    to_peer.wait_recv()
    forward = remote(ow.at[:, peer], ow.at[:, peer], sw.at[2], rw.at[2], (seq, partner))
    forward.start()
    to_peer.wait_send()
    to_partner.wait()
    for copy in copies:
        copy.wait()
    forward.wait()


def enter(rows, meta, weights, n, nh):
    dma = pltpu.SemaphoreType.DMA
    return pl.pallas_call(
        functools.partial(entry_kernel, n, nh),
        out_shape=(
            jax.ShapeDtypeStruct(rows.shape, rows.dtype),
            jax.ShapeDtypeStruct(meta.shape, meta.dtype),
            jax.ShapeDtypeStruct(
                (weights.shape[0], nh) + weights.shape[1:], weights.dtype
            ),
        ),
        in_specs=[VMEM] * 3,
        out_specs=(VMEM,) * 3,
        scratch_shapes=[
            dma((n - 1,)), dma((n - 1,)), dma((n - 1,)), dma((n - 1,)), dma((3,)), dma((3,)),
        ],
        compiler_params=comm_params(1),
        name="entry_exchange",
    )(rows, meta, weights)


def swap_kernel(nh, x_ref, o_ref, send, recv):
    seq, head = lax.axis_index("seq"), lax.axis_index("head")
    targets = others(nh, head)
    greet([(seq, to) for to in targets])
    copies = [
        remote(x_ref.at[to], o_ref.at[head], send.at[step], recv.at[step], (seq, to))
        for step, to in enumerate(targets)
    ]
    for copy in copies:
        copy.start()
    o_ref[head] = x_ref[head]
    for copy in copies:
        copy.wait()


def head_swap(x, nh):
    dma = pltpu.SemaphoreType.DMA
    return pl.pallas_call(
        functools.partial(swap_kernel, nh),
        out_shape=jax.ShapeDtypeStruct(x.shape, x.dtype),
        in_specs=[VMEM],
        out_specs=VMEM,
        scratch_shapes=[dma((nh - 1,)), dma((nh - 1,))],
        compiler_params=comm_params(2),
        name="head_swap",
    )(x)


def sum_kernel(n, x_ref, o_ref, held, send, recv, send_b, recv_b):
    seq, head = lax.axis_index("seq"), lax.axis_index("head")
    targets = others(n, seq)
    greet([(to, head) for to in targets])
    copies = [
        remote(x_ref.at[to], held.at[step], send.at[step], recv.at[step], (to, head))
        for step, to in enumerate(targets)
    ]
    for copy in copies:
        copy.start()
    total = x_ref[seq].astype(jnp.float32)
    for step, copy in enumerate(copies):
        copy.wait()
        total = total + held[step].astype(jnp.float32)
    o_ref[seq] = total.astype(o_ref.dtype)
    copies = [
        remote(o_ref.at[seq], o_ref.at[seq], send_b.at[step], recv_b.at[step], (to, head))
        for step, to in enumerate(targets)
    ]
    for copy in copies:
        copy.start()
    for copy in copies:
        copy.wait()


def seq_sum(x, n):
    dma = pltpu.SemaphoreType.DMA
    return pl.pallas_call(
        functools.partial(sum_kernel, n),
        out_shape=jax.ShapeDtypeStruct(x.shape, x.dtype),
        in_specs=[VMEM],
        out_specs=VMEM,
        scratch_shapes=[
            pltpu.VMEM((n - 1,) + x.shape[1:], x.dtype),
            dma((n - 1,)), dma((n - 1,)), dma((n - 1,)), dma((n - 1,)),
        ],
        compiler_params=comm_params(4),
        name="gradient_sum",
    )(x)


def route_kernel(nh, dest_ref, image_ref, x_ref, o_ref, m_ref, sems):
    head = lax.axis_index("head")
    part = o_ref.shape[1]
    pairs = dest_ref.shape[0] // 2
    m_ref[...] = jnp.full(m_ref.shape, -1, jnp.int32)

    def piece(pair):
        dest = dest_ref[2 * pair]
        known = jnp.maximum(dest, 0)
        offset = head * part
        slot = 2 * pair + lax.rem(known + lax.div(offset, BLK), 2)
        start = pl.multiple_of(slot * BLK + lax.rem(offset, BLK), part)
        target = lax.div(known, BLK_DEV)
        copy = pltpu.make_async_copy(x_ref.at[pl.ds(start, part)], o_ref.at[target], sems.at[pair])
        return dest, target, copy

    for pair in range(pairs):
        dest, target, copy = piece(pair)

        @pl.when(dest >= 0)
        def _():
            copy.start()
            same = (image_ref[2 * pair] == image_ref[2 * pair + 1]).astype(jnp.int32)
            code = 2 * lax.div(lax.rem(dest, BLK_DEV), 2) + same
            m_ref[target] = jnp.full(m_ref.shape[1:], code, jnp.int32)

    for pair in range(pairs):
        dest, target, copy = piece(pair)

        @pl.when(dest >= 0)
        def _():
            copy.wait()


def route(slot_dest, slot_image, patches, n, nh):
    smem = pl.BlockSpec(memory_space=pltpu.SMEM)
    part = PAIR // nh
    return pl.pallas_call(
        functools.partial(route_kernel, nh),
        out_shape=(
            jax.ShapeDtypeStruct((n, part, patches.shape[1]), patches.dtype),
            jax.ShapeDtypeStruct((n, 8, LANES), jnp.int32),
        ),
        in_specs=[smem, smem, pl.BlockSpec(memory_space=pl.ANY)],
        out_specs=(VMEM, VMEM),
        scratch_shapes=[pltpu.SemaphoreType.DMA((slot_dest.shape[0] // 2,))],
        compiler_params=pltpu.CompilerParams(vmem_limit_bytes=56 * 1024 * 1024),
        name="route_pairs",
    )(slot_dest, slot_image, patches)


def select_kernel(code_ref, x_ref, o_ref, same_ref, sems):
    head = lax.axis_index("head")
    same_ref[0] = 0

    def begin(source, carry):
        code = code_ref[source]

        @pl.when(code >= 0)
        def _():
            pair = lax.div(code, 2)
            pltpu.make_async_copy(x_ref.at[source], o_ref.at[pair], sems.at[pair]).start()

            @pl.when(pair == head)
            def _():
                same_ref[0] = lax.rem(code, 2)

        return carry

    lax.fori_loop(0, code_ref.shape[0], begin, 0)
    for pair in range(o_ref.shape[0]):
        pltpu.make_async_copy(x_ref.at[0], o_ref.at[pair], sems.at[pair]).wait()


def select(codes, arrived, pairs):
    smem = pl.BlockSpec(memory_space=pltpu.SMEM)
    return pl.pallas_call(
        select_kernel,
        out_shape=(
            jax.ShapeDtypeStruct((pairs,) + arrived.shape[1:], arrived.dtype),
            jax.ShapeDtypeStruct((1,), jnp.int32),
        ),
        in_specs=[smem, pl.BlockSpec(memory_space=pl.ANY)],
        out_specs=(VMEM, smem),
        scratch_shapes=[pltpu.SemaphoreType.DMA((pairs,))],
        compiler_params=pltpu.CompilerParams(vmem_limit_bytes=24 * 1024 * 1024),
        name="select_pairs",
    )(codes, arrived)


CHUNK = 128


def encode_kernel(
    nh, flag_ref, x_ref, w_ref, gain_ref, o_ref, q_ref, k_ref, v_ref, a_ref, send, recv
):
    seq, head = lax.axis_index("seq"), lax.axis_index("head")
    partner, peer = head_pals(nh, head)
    greet([(seq, partner), (seq, peer)])
    width = x_ref.shape[1]
    wide = x_ref[...].astype(jnp.float32)
    factor = lax.rsqrt(jnp.mean(wide * wide, axis=-1, keepdims=True) + EPSILON)
    normed = (wide * factor * gain_ref[...]).astype(jnp.bfloat16)

    def project(which):
        return lax.dot_general(
            normed, w_ref[which].reshape(width, width), NT, preferred_element_type=jnp.float32
        ).astype(jnp.bfloat16)

    q_ref[...] = project(0) * jnp.bfloat16(HDIM ** (-0.5))
    k_ref[...] = project(1)
    v_ref[...] = project(2)
    apart = jnp.where(flag_ref[0] > 0, 0.0, -1e30).astype(jnp.float32)
    key_block = lax.broadcasted_iota(jnp.int32, (1, PAIR), 1) // BLK
    first = lax.broadcasted_iota(jnp.int32, (CHUNK, LANES), 1) < HDIM
    direct = []
    forwards = []

    for chunk in range(PAIR // CHUNK):
        rows = pl.ds(chunk * CHUNK, CHUNK)
        bias = jnp.where(key_block == chunk * CHUNK // BLK, 0.0, apart)

        def slabs(index, carry):
            for inner in range(2):
                columns = pl.ds(pl.multiple_of((2 * index + inner) * LANES, LANES), LANES)
                query = q_ref[rows, columns]
                nothing = jnp.zeros_like(query)
                both = jnp.concatenate(
                    [jnp.where(first, query, nothing), jnp.where(first, nothing, query)], axis=0
                )
                scores = lax.dot_general(
                    both, k_ref[:, columns], NT, preferred_element_type=jnp.float32
                ) + bias
                top = jnp.max(scores, axis=-1, keepdims=True)
                weights = jnp.exp(scores - top)
                total = jnp.sum(weights, axis=-1, keepdims=True)
                mixed = jnp.dot(
                    weights.astype(jnp.bfloat16),
                    v_ref[:, columns],
                    preferred_element_type=jnp.float32,
                ) * (1.0 / total)
                a_ref[:, columns] = jnp.where(first, mixed[:CHUNK], mixed[CHUNK:]).astype(
                    jnp.bfloat16
                )
            return carry

        lax.fori_loop(0, width // LANES // 2, slabs, 0)
        mixed = jnp.dot(
            a_ref[...], w_ref[3].reshape(width, width), preferred_element_type=jnp.float32
        )
        o_ref[head, rows] = (x_ref[rows].astype(jnp.float32) + mixed).astype(jnp.bfloat16)
        mine = o_ref.at[head, rows]
        to_peer = remote(mine, mine, send.at[0, chunk], recv.at[0, chunk], (seq, peer))
        to_partner = remote(mine, mine, send.at[1, chunk], recv.at[1, chunk], (seq, partner))
        to_peer.start()
        to_partner.start()
        direct.append((to_peer, to_partner))
    for chunk, (to_peer, to_partner) in enumerate(direct):
        to_peer.wait_recv()
        theirs = o_ref.at[peer, pl.ds(chunk * CHUNK, CHUNK)]
        forward = remote(theirs, theirs, send.at[2, chunk], recv.at[2, chunk], (seq, partner))
        forward.start()
        forwards.append(forward)
    for (to_peer, to_partner), forward in zip(direct, forwards):
        to_peer.wait_send()
        to_partner.wait()
        forward.wait()


def encode_and_gather(flag, rows, weights, gain, nh):
    dma = pltpu.SemaphoreType.DMA
    chunks = PAIR // CHUNK
    return pl.pallas_call(
        functools.partial(encode_kernel, nh),
        out_shape=jax.ShapeDtypeStruct((nh,) + rows.shape, rows.dtype),
        in_specs=[pl.BlockSpec(memory_space=pltpu.SMEM), VMEM, VMEM, VMEM],
        out_specs=VMEM,
        scratch_shapes=[pltpu.VMEM(rows.shape, jnp.bfloat16)] * 3
        + [pltpu.VMEM((CHUNK, rows.shape[1]), jnp.bfloat16), dma((3, chunks)), dma((3, chunks))],
        compiler_params=comm_params(3),
        name="encode_and_gather",
    )(flag, rows, weights, gain)


def norm_rows(values, gain_vector):
    widened = values.astype(jnp.float32)
    factor = lax.rsqrt(jnp.mean(widened * widened, axis=-1, keepdims=True) + EPSILON)
    return (widened * factor * gain_vector).astype(jnp.bfloat16)


def renorm(updated, initial, axis):
    target_norm = jnp.sqrt(jnp.sum(initial * initial, axis=axis, keepdims=True))
    return (
        updated
        * target_norm
        * lax.rsqrt(jnp.sum(updated * updated, axis=axis, keepdims=True) + EPSILON)
    )


def to_tiles(gradient, n):
    rows, columns = gradient.shape
    flat = jnp.concatenate(
        [gradient[:, c : c + LANES] for c in range(0, columns, LANES)], axis=0
    )
    chunk = 16 * (-(-flat.shape[0] // (16 * n)))
    return jnp.pad(flat, ((0, chunk * n - flat.shape[0]), (0, 0))).reshape(n, chunk, LANES)


def from_tiles(tiles, rows, columns):
    flat = tiles.reshape(-1, LANES)
    return jnp.concatenate(
        [flat[c * rows : (c + 1) * rows] for c in range(columns // LANES)], axis=1
    )


def on_device(
    patches,
    slot_image,
    slot_dest,
    enc_gain,
    w_qkv,
    w_out,
    fast_gain,
    w_fast,
    w_rate,
    fast_gate_up,
    fast_down,
):
    n = lax.axis_size("seq")
    nh = lax.axis_size("head")
    head = lax.axis_index("head")
    width = w_out.shape[0]
    model = patches.shape[1]
    sending, meta = route(slot_dest, slot_image, patches, n, nh)
    weights = jnp.concatenate([jnp.swapaxes(w_qkv, 1, 2), w_out[None]], axis=0)
    arrived, codes, full_weights = enter(sending, meta, weights, n, nh)
    chosen, same = select(codes[:, 0, 0], arrived, BLK_DEV // 2)
    own_pair = head_swap(chosen, nh).reshape(PAIR, model)
    full_embedded = encode_and_gather(same, own_pair, full_weights, enc_gain[None, :], nh)
    full_embedded = full_embedded.reshape(nh * PAIR, model)
    embedded = lax.dynamic_slice_in_dim(full_embedded, head * width, width, 1)

    normed_fast = norm_rows(full_embedded, fast_gain)
    fast_query = jnp.dot(normed_fast, w_fast[0], preferred_element_type=jnp.float32).astype(
        jnp.bfloat16
    )
    fast_key = jnp.dot(normed_fast, w_fast[1], preferred_element_type=jnp.float32).astype(
        jnp.bfloat16
    )
    fast_value = jnp.dot(normed_fast, w_fast[2], preferred_element_type=jnp.float32).astype(
        jnp.bfloat16
    )
    token_total = embedded.shape[0] * n
    rates = (
        RATE_SCALE
        * jax.nn.softplus(jnp.dot(normed_fast, w_rate, preferred_element_type=jnp.float32))
        * token_total ** (-0.5)
    )
    gate_init = fast_gate_up[0, 0]
    up_init = fast_gate_up[0, 1]
    down_init = fast_down[0]
    gate_half = gate_init.astype(jnp.bfloat16)
    up_half = up_init.astype(jnp.bfloat16)
    down_half = down_init.astype(jnp.bfloat16)
    key_gate = jnp.dot(fast_key, gate_half, preferred_element_type=jnp.float32)
    key_up = jnp.dot(fast_key, up_half, preferred_element_type=jnp.float32)
    sigmoid_gate = jax.nn.sigmoid(key_gate)
    hidden_key = (key_gate * sigmoid_gate * key_up).astype(jnp.bfloat16)
    out_grad = (-rates * fast_value.astype(jnp.float32)).astype(jnp.bfloat16)
    grad_down = jnp.einsum("tf,th->fh", out_grad, hidden_key, preferred_element_type=jnp.float32)
    hidden_grad = jnp.dot(out_grad, down_half.T, preferred_element_type=jnp.float32)
    gate_grad = (
        hidden_grad * key_up * sigmoid_gate * (1.0 + key_gate * (1.0 - sigmoid_gate))
    ).astype(jnp.bfloat16)
    up_grad = (hidden_grad * key_gate * sigmoid_gate).astype(jnp.bfloat16)
    grad_gate = jnp.einsum("tf,th->fh", fast_key, gate_grad, preferred_element_type=jnp.float32)
    grad_up = jnp.einsum("tf,th->fh", fast_key, up_grad, preferred_element_type=jnp.float32)
    gradient = jnp.concatenate([grad_gate, grad_up, grad_down], axis=0).astype(jnp.bfloat16)
    hidden = gradient.shape[1]
    summed = from_tiles(seq_sum(to_tiles(gradient, n), n), 3 * width, hidden).astype(jnp.float32)
    new_gate = renorm(gate_init - summed[:width], gate_init, 1)
    new_up = renorm(up_init - summed[width : 2 * width], up_init, 1)
    new_down = renorm(down_init.T - summed[2 * width :], down_init.T, 0)
    applied_gate = new_gate.astype(jnp.bfloat16)
    applied_up = new_up.astype(jnp.bfloat16)
    applied_down = new_down.astype(jnp.bfloat16)
    query_gate = jnp.dot(fast_query, applied_gate, preferred_element_type=jnp.float32)
    query_up = jnp.dot(fast_query, applied_up, preferred_element_type=jnp.float32)
    query_hidden = (jax.nn.silu(query_gate) * query_up).astype(jnp.bfloat16)
    fast_out = jnp.dot(query_hidden, applied_down.T, preferred_element_type=jnp.float32)
    return (embedded.astype(jnp.float32) + fast_out).astype(jnp.bfloat16)


def solution(mesh):
    in_specs = (
        P("seq", None),
        P("seq"),
        P("seq"),
        P(),
        P(None, None, "head"),
        P("head", None),
        P(),
        P(None, None, "head"),
        P(None, "head"),
        P("head", None, None, None),
        P("head", None, None),
    )
    out_specs = P("seq", "head")
    return jax.shard_map(
        on_device, mesh=mesh, in_specs=in_specs, out_specs=out_specs, check_vma=False
    )
```

profile of v0, /device:TPU:0, one launch (start us, length us, event | category | flops | bytes accessed | tf_op | source)
XLA Modules:
  0.0 153.2 jit_solution(11574950341660618876)
XLA Ops:
  0.0 0.0 copy-start
  0.0 1.3 broadcast_in_dim.5.gain_ref
  1.3 2.5 %pad_maximum_fusion.w_ref = bf16[4,192,768]{2,1,0:T(8,128)(2,1)} fusion(bf16[1,192,768]{2,1,0:T(8,128)(2,1)} %bitcast.87, bf16[3,192,768]{2,1,0:T(8,128)(2,1)} %bitcast.86), kind=kLoop, calls=%fused_computation.21 | loop fusion | flops 589824 | bytes 2359296 | tf_op jit(solution)/shard_map/concatenate | solution.py:405
  3.8 3.2 %route_pairs.1 = (bf16[8,128,768]{2,1,0:T(8,128)(2,1)}, s32[8,8,128]{2,1,0:T(8,128)}) custom-call(s32[16]{0:T(128)} %dest_ref.1, s32[16]{0:T(128)} %image_ref.1, bf16[4096,768]{1,0:T(8,128)(2,1)} %x_ref.1), custom_call_target="tpu_custom_call" | custom-call | tf_op jit(solution)/shard_map/route_pairs/pallas_call | solution.py:208
  7.0 40.3 %entry_exchange.1 = (bf16[8,128,768]{2,1,0:T(8,128)(2,1)}, s32[8,8,128]{2,1,0:T(8,128)}, bf16[4,4,192,768]{3,2,1,0:T(8,128)(2,1)}) custom-call(bf16[8,128,768]{2,1,0:T(8,128)(2,1)} %get-tuple-element.12.x_ref, s32[8,8,128]{2,1,0:T(8,128)} %get-tuple-element.13.m_ref, bf16[4,192,768]{2,1,0:T(8,128)(2,1)} %pad_maximum_fusion.w_ref), custom_call_target="tpu_custom_call" | custom-call | tf_op jit(solution)/shard_map/entry_exchange/pallas_call | solution.py:83
  47.3 1.0 slice_reduce_fusion.code_ref
  48.3 0.0 copy-start.1
  48.3 1.4 copy-done.1
  49.7 2.2 %select_pairs.1 = (bf16[4,128,768]{2,1,0:T(8,128)(2,1)S(1)}, s32[1]{0:T(128)}) custom-call(s32[8]{0:T(128)S(1)} %slice_reduce_fusion.code_ref, bf16[8,128,768]{2,1,0:T(8,128)(2,1)S(1)} %copy-done.1), custom_call_target="tpu_custom_call" | custom-call | tf_op jit(solution)/shard_map/select_pairs/pallas_call | solution.py:247
  51.9 0.0 copy-start.2
  51.9 0.9 copy-done.2
  52.8 11.6 %head_swap.1 = bf16[4,128,768]{2,1,0:T(8,128)(2,1)} custom-call(bf16[4,128,768]{2,1,0:T(8,128)(2,1)} %copy-done.2), custom_call_target="tpu_custom_call" | custom-call | tf_op jit(solution)/shard_map/head_swap/pallas_call | solution.py:119
  64.4 31.2 %encode_and_gather.1 = bf16[4,512,768]{2,1,0:T(8,128)(2,1)} custom-call(s32[1]{0:T(128)} %get-tuple-element.16.flag_ref, bf16[512,768]{1,0:T(8,128)(2,1)} %bitcast.83, bf16[4,4,192,768]{3,2,1,0:T(8,128)(2,1)} %get-tuple-element.18.w_ref, f32[1,768]{1,0:T(1,128)} %broadcast_in_dim.5.gain_ref), custom_call_target="tpu_custom_call" | custom-call | tf_op jit(solution)/shard_map/encode_and_gather/pallas_call | solution.py:343
  95.6 0.0 copy-start.3
  95.6 0.0 copy-start.7
  95.6 2.7 %fusion = f32[4,512]{1,0:T(4,128)S(1)} fusion(bf16[4,512,768]{2,1,0:T(8,128)(2,1)} %encode_and_gather.1), kind=kLoop, calls=%fused_computation.2 | loop fusion | flops 4716544 | bytes 3153920 | tf_op jit(solution)/shard_map/reduce_sum | solution.py:357
  98.4 0.1 copy-done.3
  98.5 1.4 constant_dynamic-slice_fusion
  99.9 2.2 %copy.14 = bf16[2048,192]{0,1:T(8,128)(2,1)} copy(bf16[2048,192]{1,0:T(8,128)(2,1)} %constant_dynamic-slice_fusion) | data formatting | bytes 1572864
  102.1 0.0 copy-done.7
  102.1 0.8 fusion.2
  102.9 0.0 copy-start.8
  102.9 0.0 copy-done
  102.9 0.9 fusion.51
  103.8 0.2 copy-done.8
  104.0 1.2 fusion.6
  105.2 1.2 convolution_convert_fusion.1
  106.4 0.0 copy-start.4
  106.4 1.2 convolution_convert_fusion.2
  107.6 0.0 copy-done.4
  107.6 0.8 fusion.28
  108.3 0.8 fusion.30
  109.1 0.0 copy-start.5
  109.1 1.1 fusion.10
  110.3 0.0 copy-done.5
  110.3 0.7 fusion.48
  111.0 1.5 fusion.12
  112.5 1.1 fusion.11
  113.7 0.1 fusion.47
  113.7 0.8 fusion.17
  114.5 30.4 %gradient_sum.1 = bf16[8,224,128]{2,1,0:T(8,128)(2,1)} custom-call(bf16[8,224,128]{2,1,0:T(8,128)(2,1)} %bitcast.84), custom_call_target="tpu_custom_call" | custom-call | tf_op jit(solution)/shard_map/gradient_sum/pallas_call | solution.py:157
  145.0 1.1 fusion.46
  146.0 0.1 maximum_convert_fusion
  146.1 0.0 copy-start.6
  146.1 0.2 multiply_reduce_fusion.1
  146.4 2.5 %fusion.27 = f32[2048,384]{1,0:T(8,128)} fusion(bf16[2048,192]{0,1:T(8,128)(2,1)S(1)} %convolution_convert_fusion.2, f32[192]{0:T(256)S(1)} %get-tuple-element.32, f32[192]{0:T(256)S(1)} %sqrt.24, f32[576,384]{1,0:T(8,128)S(1)} %maximum_convert_fusion, f32[1,2,192,384]{3,2,1,0:T(8,128)S(1)} %copy-done.4), kind=kOutput, calls=%fused_computation.57 | convolution fusion | flops 302284800 | bytes 4524032 | tf_op jit(solution)/shard_map/dot_general | solution.py:457
  148.9 0.0 copy-done.6
  148.9 4.3 %fusion.3 = bf16[2048,192]{0,1:T(8,128)(2,1)} fusion(bf16[2048,192]{0,1:T(8,128)(2,1)S(1)} %copy-done.6, f32[2048,384]{1,0:T(8,128)} %fusion.27, bf16[2048,192]{0,1:T(8,128)(2,1)S(1)} %convolution_convert_fusion.2, f32[384]{0:T(512)S(1)} %add_rsqrt_fusion.1, f32[384]{0:T(512)S(1)} %sqrt.26, f32[192]{0:T(256)S(1)} %get-tuple-element.31, f32[192]{0:T(256)S(1)} %sqrt.25, ...), kind=kOutput, calls=%fused_computation.11 | convolution fusion | flops 610467840 | bytes 6690816 | tf_op jit(solution)/shard_map/dot_general | solution.py:460
  (8 shorter events, 0.1 us)
Async XLA Ops:
  0.0 102.9 %copy-start = (bf16[768,1]{0,1:T(2,128)(2,1)S(1)}, bf16[768,1]{0,1:T(2,128)(2,1)}, u32[]{:S(2)}) copy-start(bf16[768,1]{0,1:T(2,128)(2,1)} %param.19) | copy-start | bytes 4612
  48.3 1.4 copy-start.1
  51.9 0.9 copy-start.2
  95.6 2.8 %copy-start.3 = (bf16[4,512,768]{2,1,0:T(8,128)(2,1)S(1)}, bf16[4,512,768]{2,1,0:T(8,128)(2,1)}, u32[]{:S(2)}) copy-start(bf16[4,512,768]{2,1,0:T(8,128)(2,1)} %encode_and_gather.1) | copy-start | bytes 9437188
  95.6 6.4 %copy-start.7 = (f32[768]{0:T(1024)S(1)}, f32[768]{0:T(1024)}, u32[]{:S(2)}) copy-start(f32[768]{0:T(1024)} %param.17) | copy-start | bytes 9220
  102.9 1.2 copy-start.8
  106.4 1.2 copy-start.4
  109.1 1.2 copy-start.5
  146.1 2.8 %copy-start.6 = (bf16[2048,192]{0,1:T(8,128)(2,1)S(1)}, bf16[2048,192]{0,1:T(8,128)(2,1)}, u32[]{:S(2)}) copy-start(bf16[2048,192]{0,1:T(8,128)(2,1)} %copy.14) | copy-start | bytes 2359300
where the time goes:
time: 156 us; the launch traced here: 153 us
  Pallas kernels  119 us (76%)
  matrix products  17.2 us (11%)
  local copies, waits for them, and re-layouts  9.67 us (6%)
  other arithmetic  7.2 us (5%)
    pallas_call x1, Pallas kernels, enter(): pl.pallas_call(functools.partial(entry_kernel, n, nh), out_shape=(jax.Sha...  40.3 us
    pallas_call x1, Pallas kernels, encode_and_gather(): pl.pallas_call(functools.partial(encode_kernel, nh), out_shape=jax.ShapeD...  31.2 us
    pallas_call x1, Pallas kernels, seq_sum(): pl.pallas_call(functools.partial(sum_kernel, n), out_shape=jax.ShapeDtype...  30.4 us
    pallas_call x1, Pallas kernels, head_swap(): pl.pallas_call(functools.partial(swap_kernel, nh), out_shape=jax.ShapeDty...  11.6 us
    unnamed x19, local copies, waits for them, and re-layouts  4.77 us
    dot_general x1, matrix products, on_device(): jnp.dot(query_hidden, applied_down.T, preferred_element_type=jnp.float32)  4.34 us
    pallas_call x1, Pallas kernels, route(): pl.pallas_call(functools.partial(route_kernel, nh), out_shape=(jax.ShapeD...  3.17 us

commit v1 on v0

--- a/solution.py
+++ b/solution.py
@@ -127,47 +127,6 @@
     )(x)
 
 
-def sum_kernel(n, x_ref, o_ref, held, send, recv, send_b, recv_b):
-    seq, head = lax.axis_index("seq"), lax.axis_index("head")
-    targets = others(n, seq)
-    greet([(to, head) for to in targets])
-    copies = [
-        remote(x_ref.at[to], held.at[step], send.at[step], recv.at[step], (to, head))
-        for step, to in enumerate(targets)
-    ]
-    for copy in copies:
-        copy.start()
-    total = x_ref[seq].astype(jnp.float32)
-    for step, copy in enumerate(copies):
-        copy.wait()
-        total = total + held[step].astype(jnp.float32)
-    o_ref[seq] = total.astype(o_ref.dtype)
-    copies = [
-        remote(o_ref.at[seq], o_ref.at[seq], send_b.at[step], recv_b.at[step], (to, head))
-        for step, to in enumerate(targets)
-    ]
-    for copy in copies:
-        copy.start()
-    for copy in copies:
-        copy.wait()
-
-
-def seq_sum(x, n):
-    dma = pltpu.SemaphoreType.DMA
-    return pl.pallas_call(
-        functools.partial(sum_kernel, n),
-        out_shape=jax.ShapeDtypeStruct(x.shape, x.dtype),
-        in_specs=[VMEM],
-        out_specs=VMEM,
-        scratch_shapes=[
-            pltpu.VMEM((n - 1,) + x.shape[1:], x.dtype),
-            dma((n - 1,)), dma((n - 1,)), dma((n - 1,)), dma((n - 1,)),
-        ],
-        compiler_params=comm_params(4),
-        name="gradient_sum",
-    )(x)
-
-
 def route_kernel(nh, dest_ref, image_ref, x_ref, o_ref, m_ref, sems):
     head = lax.axis_index("head")
     part = o_ref.shape[1]
@@ -352,10 +311,16 @@
     )(flag, rows, weights, gain)
 
 
-def norm_rows(values, gain_vector):
-    widened = values.astype(jnp.float32)
-    factor = lax.rsqrt(jnp.mean(widened * widened, axis=-1, keepdims=True) + EPSILON)
-    return (widened * factor * gain_vector).astype(jnp.bfloat16)
+UNIT = 256
+TT = (((0,), (0,)), ((), ()))
+
+
+def dot(a, b):
+    return jnp.dot(a, b, preferred_element_type=jnp.float32)
+
+
+def dot_nt(a, b):
+    return lax.dot_general(a, b, NT, preferred_element_type=jnp.float32)
 
 
 def renorm(updated, initial, axis):
@@ -367,20 +332,221 @@
     )
 
 
-def to_tiles(gradient, n):
-    rows, columns = gradient.shape
-    flat = jnp.concatenate(
-        [gradient[:, c : c + LANES] for c in range(0, columns, LANES)], axis=0
-    )
-    chunk = 16 * (-(-flat.shape[0] // (16 * n)))
-    return jnp.pad(flat, ((0, chunk * n - flat.shape[0]), (0, 0))).reshape(n, chunk, LANES)
-
-
-def from_tiles(tiles, rows, columns):
-    flat = tiles.reshape(-1, LANES)
-    return jnp.concatenate(
-        [flat[c * rows : (c + 1) * rows] for c in range(columns // LANES)], axis=1
-    )
+def fast_kernel(
+    n, e_ref, wf_ref, wr_ref, gu_ref, dn_ref, gain_ref, o_ref,
+    w_s, q_s, k_s, kt_s, og_s, ogt_s, col_s, pair_s, hk_s, guw_s, dnh_s, dn_s, g_s, sum_s, ag_s, ad_s,
+    part_s, xin_s, half_s, zin_s, res_s,
+    xs, xr, zs, zr, rs, rr, fs, fr,
+):
+    seq, head = lax.axis_index("seq"), lax.axis_index("head")
+    inner_count, outer_count = 2, n // 2
+    inner, outer = lax.rem(seq, 2), lax.div(seq, 2)
+    side = (outer * 2 + 1 - inner, head)
+    lane = [(lax.rem(outer + step, outer_count) * 2 + inner, head) for step in range(1, outer_count)]
+    greet([side] + lane)
+    tokens, model = e_ref.shape
+    width, hidden = gu_ref.shape[1:]
+    wide = k_s.shape[1]
+    parts = hidden // LANES
+    chunk = part_s.shape[3]
+    bf, f32 = jnp.bfloat16, jnp.float32
+
+    w_s[...] = jnp.zeros_like(w_s)
+    for which in range(3):
+        w_s[:, which * wide : which * wide + width] = wf_ref[which]
+    rate_at = 2 * wide + width
+    w_s[:, rate_at : rate_at + 1] = wr_ref[...]
+    guw_s[...] = jnp.zeros_like(guw_s)
+    dnh_s[...] = jnp.zeros_like(dnh_s)
+    dn_s[...] = jnp.zeros_like(dn_s)
+    dn_s[:, :width] = dn_ref[...]
+    dnh_s[...] = dn_s[...].astype(bf)
+    g_s[...] = jnp.zeros_like(g_s)
+    for part in range(parts):
+        cut = slice(part * LANES, (part + 1) * LANES)
+        guw_s[part, :width, :LANES] = gu_ref[0, :, cut].astype(bf)
+        guw_s[part, :width, LANES:] = gu_ref[1, :, cut].astype(bf)
+
+    for which in range(model // width):
+
+        @pl.when(head == which)
+        def _():
+            col_s[...] = e_ref[:, which * width : (which + 1) * width]
+
+    token_total = tokens * n
+
+    def project(unit, carry):
+        rows = pl.ds(pl.multiple_of(unit * UNIT, UNIT), UNIT)
+        wide_rows = e_ref[rows].astype(f32)
+        factor = lax.rsqrt(jnp.mean(wide_rows * wide_rows, axis=-1, keepdims=True) + EPSILON)
+        normed = (wide_rows * factor * gain_ref[...]).astype(bf)
+        mapped = dot(normed, w_s[...])
+        q_s[rows] = mapped[:, :wide].astype(bf)
+        key = mapped[:, wide : 2 * wide].astype(bf)
+        k_s[rows] = key
+        kt_s[:, rows] = key.T
+        value = mapped[:, 2 * wide :].astype(bf).astype(f32)
+        before = mapped[:, rate_at : rate_at + 1]
+        soft = jnp.maximum(before, 0.0) + jnp.log1p(jnp.exp(-jnp.abs(before)))
+        rate = (RATE_SCALE * token_total ** (-0.5)) * soft
+        back = (-rate * value).astype(bf)
+        og_s[rows] = back
+        ogt_s[:, rows] = back.T
+        return carry
+
+    lax.fori_loop(0, tokens // UNIT, project, 0)
+
+    def compute(part):
+        def body(unit, carry):
+            rows = pl.ds(pl.multiple_of(unit * UNIT, UNIT), UNIT)
+            both = dot(k_s[rows], guw_s[part])
+            gate, up = both[:, :LANES], both[:, LANES:]
+            grad = dot_nt(og_s[rows], dnh_s[part * LANES : (part + 1) * LANES])
+            sig = jax.nn.sigmoid(gate)
+            silu = gate * sig
+            hk_s[rows] = (silu * up).astype(bf)
+            pair_s[rows, :LANES] = (grad * up * sig * (1.0 + gate * (1.0 - sig))).astype(bf)
+            pair_s[rows, LANES:] = (grad * silu).astype(bf)
+            return carry
+
+        lax.fori_loop(0, tokens // UNIT, body, 0)
+        first = dot(kt_s[...], pair_s[...])
+        second = dot(ogt_s[...], hk_s[...])
+        g_s[0:width] = first[:width, :LANES]
+        g_s[width : 2 * width] = first[:width, LANES:]
+        g_s[2 * width : 3 * width] = second[:width]
+        for i in range(inner_count):
+            for o in range(outer_count):
+                at = (i * outer_count + o) * chunk
+                part_s[part, i, o] = g_s[at : at + chunk].astype(bf)
+
+    def x_copy(part):
+        return remote(part_s.at[part, 1 - inner], xin_s.at[part], xs.at[part], xr.at[part], side)
+
+    def z_copies(part):
+        return [
+            remote(
+                half_s.at[part, lax.rem(outer + step, outer_count)], zin_s.at[part, step - 1],
+                zs.at[part, step - 1], zr.at[part, step - 1], lane[step - 1],
+            )
+            for step in range(1, outer_count)
+        ]
+
+    def r_copies(part):
+        mine = res_s.at[part, inner, outer]
+        return [
+            remote(mine, mine, rs.at[part, step], rr.at[part, step], to)
+            for step, to in enumerate(lane + [side])
+        ]
+
+    def f_copy(part, step):
+        theirs = res_s.at[part, inner, lax.rem(outer + outer_count - step, outer_count)]
+        return remote(theirs, theirs, fs.at[part, step - 1], fr.at[part, step - 1], side)
+
+    def stage_x(part):
+        x_copy(part).start()
+
+    def stage_z(part):
+        x_copy(part).wait_recv()
+        for o in range(outer_count):
+            half_s[part, o] = (
+                part_s[part, inner, o].astype(f32) + xin_s[part, o].astype(f32)
+            ).astype(bf)
+        for copy in z_copies(part):
+            copy.start()
+
+    def stage_r(part):
+        total = half_s[part, outer].astype(f32)
+        for step, copy in enumerate(z_copies(part)):
+            copy.wait_recv()
+            total = total + zin_s[part, step].astype(f32)
+        res_s[part, inner, outer] = total.astype(bf)
+        for copy in r_copies(part):
+            copy.start()
+
+    def stage_f(part):
+        copies = r_copies(part)
+        for step in range(1, outer_count):
+            copies[step - 1].wait_recv()
+            f_copy(part, step).start()
+
+    def finish(part):
+        r_copies(part)[-1].wait_recv()
+        for step in range(1, outer_count):
+            f_copy(part, step).wait_recv()
+
+    stages = [stage_x, stage_z, stage_r, stage_f]
+    for tick in range(parts + len(stages) - 1):
+        if tick < parts:
+            compute(tick)
+        for which, stage in enumerate(stages):
+            if 0 <= tick - which < parts:
+                stage(tick - which)
+    for part in range(parts):
+        finish(part)
+        cut = slice(part * LANES, (part + 1) * LANES)
+        for i in range(inner_count):
+            for o in range(outer_count):
+                at = (i * outer_count + o) * chunk
+                sum_s[at : at + chunk, cut] = res_s[part, i, o].astype(f32)
+    for part in range(parts):
+        x_copy(part).wait_send()
+        for copy in z_copies(part) + r_copies(part):
+            copy.wait_send()
+        for step in range(1, outer_count):
+            f_copy(part, step).wait_send()
+
+    ag_s[...] = jnp.zeros_like(ag_s)
+    for which in range(2):
+        start = gu_ref[which]
+        fresh = renorm(start - sum_s[which * width : (which + 1) * width], start, 1)
+        ag_s[:width, which * hidden : (which + 1) * hidden] = fresh.astype(bf)
+    start = dn_s[...].T[:width]
+    ad_s[...] = renorm(start - sum_s[2 * width : 3 * width], start, 0).astype(bf)
+
+    def final(unit, carry):
+        rows = pl.ds(pl.multiple_of(unit * UNIT, UNIT), UNIT)
+        both = dot(q_s[rows], ag_s[...])
+        gate = both[:, :hidden]
+        inside = (gate * jax.nn.sigmoid(gate) * both[:, hidden:]).astype(bf)
+        o_ref[rows] = (col_s[rows].astype(f32) + dot_nt(inside, ad_s[...])).astype(bf)
+        return carry
+
+    lax.fori_loop(0, tokens // UNIT, final, 0)
+
+
+def fast_update(embedded, w_fast, w_rate, gate_up, down, gain, n):
+    tokens, model = embedded.shape
+    width, hidden = gate_up.shape[1:]
+    wide = LANES * (-(-width // LANES))
+    parts = hidden // LANES
+    chunk = 8 * (-(-3 * width // (8 * n)))
+    rows = max(3 * width, chunk * n)
+    bf, f32 = jnp.bfloat16, jnp.float32
+    vmem, dma = pltpu.VMEM, pltpu.SemaphoreType.DMA
+    outer = n // 2
+    return pl.pallas_call(
+        functools.partial(fast_kernel, n),
+        out_shape=jax.ShapeDtypeStruct((tokens, width), bf),
+        in_specs=[VMEM] * 6,
+        out_specs=VMEM,
+        scratch_shapes=[
+            vmem((model, 3 * wide), bf),
+            vmem((tokens, wide), bf), vmem((tokens, wide), bf), vmem((wide, tokens), bf),
+            vmem((tokens, wide), bf), vmem((wide, tokens), bf), vmem((tokens, width), bf),
+            vmem((tokens, 2 * LANES), bf), vmem((tokens, LANES), bf),
+            vmem((parts, wide, 2 * LANES), bf), vmem((hidden, wide), bf), vmem((hidden, wide), f32),
+            vmem((rows, LANES), f32), vmem((rows, hidden), f32),
+            vmem((wide, 2 * hidden), bf), vmem((width, hidden), bf),
+            vmem((parts, 2, outer, chunk, LANES), bf), vmem((parts, outer, chunk, LANES), bf),
+            vmem((parts, outer, chunk, LANES), bf), vmem((parts, outer - 1, chunk, LANES), bf),
+            vmem((parts, 2, outer, chunk, LANES), bf),
+            dma((parts,)), dma((parts,)), dma((parts, outer - 1)), dma((parts, outer - 1)),
+            dma((parts, outer)), dma((parts, outer)), dma((parts, outer - 1)), dma((parts, outer - 1)),
+        ],
+        compiler_params=comm_params(4),
+        name="fast_update",
+    )(embedded, w_fast, w_rate, gate_up, down, gain)
 
 
 def on_device(
@@ -399,7 +565,6 @@
     n = lax.axis_size("seq")
     nh = lax.axis_size("head")
     head = lax.axis_index("head")
-    width = w_out.shape[0]
     model = patches.shape[1]
     sending, meta = route(slot_dest, slot_image, patches, n, nh)
     weights = jnp.concatenate([jnp.swapaxes(w_qkv, 1, 2), w_out[None]], axis=0)
@@ -408,57 +573,9 @@
     own_pair = head_swap(chosen, nh).reshape(PAIR, model)
     full_embedded = encode_and_gather(same, own_pair, full_weights, enc_gain[None, :], nh)
     full_embedded = full_embedded.reshape(nh * PAIR, model)
-    embedded = lax.dynamic_slice_in_dim(full_embedded, head * width, width, 1)
-
-    normed_fast = norm_rows(full_embedded, fast_gain)
-    fast_query = jnp.dot(normed_fast, w_fast[0], preferred_element_type=jnp.float32).astype(
-        jnp.bfloat16
+    return fast_update(
+        full_embedded, w_fast, w_rate, fast_gate_up[0], fast_down[0], fast_gain[None, :], n
     )
-    fast_key = jnp.dot(normed_fast, w_fast[1], preferred_element_type=jnp.float32).astype(
-        jnp.bfloat16
-    )
-    fast_value = jnp.dot(normed_fast, w_fast[2], preferred_element_type=jnp.float32).astype(
-        jnp.bfloat16
-    )
-    token_total = embedded.shape[0] * n
-    rates = (
-        RATE_SCALE
-        * jax.nn.softplus(jnp.dot(normed_fast, w_rate, preferred_element_type=jnp.float32))
-        * token_total ** (-0.5)
-    )
-    gate_init = fast_gate_up[0, 0]
-    up_init = fast_gate_up[0, 1]
-    down_init = fast_down[0]
-    gate_half = gate_init.astype(jnp.bfloat16)
-    up_half = up_init.astype(jnp.bfloat16)
-    down_half = down_init.astype(jnp.bfloat16)
-    key_gate = jnp.dot(fast_key, gate_half, preferred_element_type=jnp.float32)
-    key_up = jnp.dot(fast_key, up_half, preferred_element_type=jnp.float32)
-    sigmoid_gate = jax.nn.sigmoid(key_gate)
-    hidden_key = (key_gate * sigmoid_gate * key_up).astype(jnp.bfloat16)
-    out_grad = (-rates * fast_value.astype(jnp.float32)).astype(jnp.bfloat16)
-    grad_down = jnp.einsum("tf,th->fh", out_grad, hidden_key, preferred_element_type=jnp.float32)
-    hidden_grad = jnp.dot(out_grad, down_half.T, preferred_element_type=jnp.float32)
-    gate_grad = (
-        hidden_grad * key_up * sigmoid_gate * (1.0 + key_gate * (1.0 - sigmoid_gate))
-    ).astype(jnp.bfloat16)
-    up_grad = (hidden_grad * key_gate * sigmoid_gate).astype(jnp.bfloat16)
-    grad_gate = jnp.einsum("tf,th->fh", fast_key, gate_grad, preferred_element_type=jnp.float32)
-    grad_up = jnp.einsum("tf,th->fh", fast_key, up_grad, preferred_element_type=jnp.float32)
-    gradient = jnp.concatenate([grad_gate, grad_up, grad_down], axis=0).astype(jnp.bfloat16)
-    hidden = gradient.shape[1]
-    summed = from_tiles(seq_sum(to_tiles(gradient, n), n), 3 * width, hidden).astype(jnp.float32)
-    new_gate = renorm(gate_init - summed[:width], gate_init, 1)
-    new_up = renorm(up_init - summed[width : 2 * width], up_init, 1)
-    new_down = renorm(down_init.T - summed[2 * width :], down_init.T, 0)
-    applied_gate = new_gate.astype(jnp.bfloat16)
-    applied_up = new_up.astype(jnp.bfloat16)
-    applied_down = new_down.astype(jnp.bfloat16)
-    query_gate = jnp.dot(fast_query, applied_gate, preferred_element_type=jnp.float32)
-    query_up = jnp.dot(fast_query, applied_up, preferred_element_type=jnp.float32)
-    query_hidden = (jax.nn.silu(query_gate) * query_up).astype(jnp.bfloat16)
-    fast_out = jnp.dot(query_hidden, applied_down.T, preferred_element_type=jnp.float32)
-    return (embedded.astype(jnp.float32) + fast_out).astype(jnp.bfloat16)
 
 
 def solution(mesh):

time: 156 us -> 148 us (0.949); the launches traced: 153 us -> 147 us
  matrix products: 17.2 us -> 0 us
  Pallas kernels: 119 us -> 136 us
  other arithmetic: 7.2 us -> 1.21 us
    dot_general x12 -> x0, matrix products: 17.2 us -> none  [the longest x1 4.34 us: on_device(): jnp.dot(query_hidden, applied_down.T, preferred_element_type=jnp.float32)]
    pallas_call x1, Pallas kernels: 30.4 us -> 47.5 us  [fast_update(): pl.pallas_call(functools.partial(fast_kernel, n), out_shape=jax.ShapeDtyp...]
    reduce_sum x2 -> x0, other arithmetic: 2.97 us -> none  [the longest x1 2.73 us: norm_rows(): jnp.mean(widened * widened, axis=-1, keepdims=True) + EPSILON]
    pallas_call x0 -> x1, local copies, waits for them, and re-layouts: none -> 2.19 us  [fast_update(): pl.pallas_call(functools.partial(fast_kernel, n), out_shape=jax.ShapeDtyp...]
    unnamed x19 -> x21, local copies, waits for them, and re-layouts: 4.77 us -> 5.5 us
where the time goes in v1:
time: 148 us; the launch traced here: 147 us
  Pallas kernels  136 us (92%)
  local copies, waits for them, and re-layouts  9.84 us (7%)
    pallas_call x1, Pallas kernels, fast_update(): pl.pallas_call(functools.partial(fast_kernel, n), out_shape=jax.ShapeDtyp...  47.5 us
    pallas_call x1, Pallas kernels, enter(): pl.pallas_call(functools.partial(entry_kernel, n, nh), out_shape=(jax.Sha...  40.2 us
    pallas_call x1, Pallas kernels, encode_and_gather(): pl.pallas_call(functools.partial(encode_kernel, nh), out_shape=jax.ShapeD...  31.3 us
    pallas_call x1, Pallas kernels, head_swap(): pl.pallas_call(functools.partial(swap_kernel, nh), out_shape=jax.ShapeDty...  11.6 us
    unnamed x21, local copies, waits for them, and re-layouts  5.5 us
    pallas_call x1, Pallas kernels, route(): pl.pallas_call(functools.partial(route_kernel, nh), out_shape=(jax.ShapeD...  3.32 us

profile of v1, /device:TPU:0, one launch (start us, length us, event | category | flops | bytes accessed | tf_op | source)
XLA Modules:
  0.0 147.4 jit_solution(5892434733334064695)
XLA Ops:
  0.0 0.0 copy-start.2
  0.0 0.0 copy-start.4
  0.0 3.3 %route_pairs.1 = (bf16[8,128,768]{2,1,0:T(8,128)(2,1)}, s32[8,8,128]{2,1,0:T(8,128)}) custom-call(s32[16]{0:T(128)} %dest_ref.1, s32[16]{0:T(128)} %image_ref.1, bf16[4096,768]{1,0:T(8,128)(2,1)} %x_ref.1), custom_call_target="tpu_custom_call" | custom-call | tf_op jit(solution)/shard_map/route_pairs/pallas_call | solution.py:167
  3.3 0.0 copy-done.2
  3.3 0.0 copy-done.4
  3.3 1.2 pad_maximum_fusion.w_ref
  4.6 40.2 %entry_exchange.1 = (bf16[8,128,768]{2,1,0:T(8,128)(2,1)}, s32[8,8,128]{2,1,0:T(8,128)}, bf16[4,4,192,768]{3,2,1,0:T(8,128)(2,1)}) custom-call(bf16[8,128,768]{2,1,0:T(8,128)(2,1)} %get-tuple-element.12.x_ref, s32[8,8,128]{2,1,0:T(8,128)} %get-tuple-element.13.m_ref, bf16[4,192,768]{2,1,0:T(8,128)(2,1)} %pad_maximum_fusion.w_ref), custom_call_target="tpu_custom_call" | custom-call | tf_op jit(solution)/shard_map/entry_exchange/pallas_call | solution.py:83
  44.8 1.0 slice_reduce_fusion.code_ref
  45.8 0.0 copy-start
  45.8 1.4 copy-done
  47.2 0.0 copy-start.6
  47.2 2.2 %select_pairs.1 = (bf16[4,128,768]{2,1,0:T(8,128)(2,1)S(1)}, s32[1]{0:T(128)}) custom-call(s32[8]{0:T(128)S(1)} %slice_reduce_fusion.code_ref, bf16[8,128,768]{2,1,0:T(8,128)(2,1)S(1)} %copy-done), custom_call_target="tpu_custom_call" | custom-call | tf_op jit(solution)/shard_map/select_pairs/pallas_call | solution.py:206
  49.4 0.0 copy-start.1
  49.5 0.9 copy-done.1
  50.3 11.6 %head_swap.1 = bf16[4,128,768]{2,1,0:T(8,128)(2,1)} custom-call(bf16[4,128,768]{2,1,0:T(8,128)(2,1)} %copy-done.1), custom_call_target="tpu_custom_call" | custom-call | tf_op jit(solution)/shard_map/head_swap/pallas_call | solution.py:119
  61.9 0.0 copy-done.6
  62.0 0.6 broadcast_in_dim.10.gain_ref
  62.5 0.0 copy-start.3
  62.5 31.3 %encode_and_gather.1 = bf16[4,512,768]{2,1,0:T(8,128)(2,1)} custom-call(s32[1]{0:T(128)} %get-tuple-element.16.flag_ref, bf16[512,768]{1,0:T(8,128)(2,1)} %bitcast.7, bf16[4,4,192,768]{3,2,1,0:T(8,128)(2,1)} %get-tuple-element.18.w_ref, f32[1,768]{1,0:T(1,128)} %broadcast_in_dim.10.gain_ref), custom_call_target="tpu_custom_call" | custom-call | tf_op jit(solution)/shard_map/encode_and_gather/pallas_call | solution.py:302
  93.8 0.0 copy-start.5
  93.8 0.0 copy-start.8
  93.9 0.0 copy-start.7
  93.9 0.0 copy-done.3
  93.9 1.4 copy.17.wf_ref
  95.3 0.0 copy-done.5
  95.3 0.9 copy.16
  96.2 0.0 copy-done.8
  96.2 0.8 copy.18.wr_ref
  97.1 0.0 copy-done.7
  97.1 0.6 broadcast_in_dim.11.gain_ref
  97.7 47.5 %fast_update.1 = bf16[2048,192]{1,0:T(8,128)(2,1)} custom-call(bf16[2048,768]{1,0:T(8,128)(2,1)} %bitcast.6, bf16[3,768,192]{2,1,0:T(8,128)(2,1)} %copy.17.wf_ref, bf16[768,1]{1,0:T(8,128)(2,1)} %copy.18.wr_ref, f32[2,192,384]{2,1,0:T(8,128)} %bitcast.10, f32[384,192]{1,0:T(8,128)} %bitcast.8, f32[1,768]{1,0:T(1,128)} %broadcast_in_dim.11.gain_ref), custom_call_target="tpu_custom_call" | custom-call | tf_op jit(solution)/shard_map/fast_update/pallas_call | solution.py:528
  145.2 2.2 %copy.19 = bf16[2048,192]{0,1:T(8,128)(2,1)} copy(bf16[2048,192]{1,0:T(8,128)(2,1)} %fast_update.1) | data formatting | bytes 1572864 | tf_op jit(solution)/shard_map/fast_update/pallas_call | solution.py:528
Async XLA Ops:
  0.0 3.3 %copy-start.2 = (bf16[3,768,192]{1,2,0:T(8,128)(2,1)S(1)}, bf16[3,768,192]{1,2,0:T(8,128)(2,1)}, u32[]{:S(2)}) copy-start(bf16[3,768,192]{1,2,0:T(8,128)(2,1)} %param.15) | copy-start | bytes 2654212
  0.0 3.3 %copy-start.4 = (bf16[192,768]{1,0:T(8,128)(2,1)S(1)}, bf16[192,768]{1,0:T(8,128)(2,1)}, u32[]{:S(2)}) copy-start(bf16[192,768]{1,0:T(8,128)(2,1)} %param.16) | copy-start | bytes 884740
  45.8 1.4 copy-start
  47.2 14.7 %copy-start.6 = (f32[768]{0:T(1024)S(1)}, f32[768]{0:T(1024)}, u32[]{:S(2)}) copy-start(f32[768]{0:T(1024)} %param.14) | copy-start | bytes 9220
  49.4 0.9 copy-start.1
  62.5 31.3 %copy-start.3 = (bf16[3,768,192]{1,2,0:T(8,128)(2,1)S(1)}, bf16[3,768,192]{1,2,0:T(8,128)(2,1)}, u32[]{:S(2)}) copy-start(bf16[3,768,192]{1,2,0:T(8,128)(2,1)} %param.18) | copy-start | bytes 2654212
  93.8 1.5 %copy-start.5 = (f32[1,384,192]{1,2,0:T(8,128)S(1)}, f32[1,384,192]{1,2,0:T(8,128)}, u32[]{:S(2)}) copy-start(f32[1,384,192]{1,2,0:T(8,128)} %param.21) | copy-start | bytes 884740
  93.8 2.4 %copy-start.8 = (bf16[768,1]{0,1:T(2,128)(2,1)S(1)}, bf16[768,1]{0,1:T(2,128)(2,1)}, u32[]{:S(2)}) copy-start(bf16[768,1]{0,1:T(2,128)(2,1)} %param.19) | copy-start | bytes 4612
  93.9 3.2 %copy-start.7 = (f32[768]{0:T(1024)S(1)}, f32[768]{0:T(1024)}, u32[]{:S(2)}) copy-start(f32[768]{0:T(1024)} %param.17) | copy-start | bytes 9220

commit v2 on v0

v2 whole, which is shorter than its diff:
```python
import functools
import types

import jax
import jax.numpy as jnp
from jax import lax
from jax.experimental import pallas as pl
from jax.experimental.pallas import tpu as pltpu
from jax.sharding import PartitionSpec as P

HDIM = 64
BLK = 256
BLK_DEV = 8
PAIR = 2 * BLK
EPSILON = 1e-06
RATE_SCALE = 0.1
LANES = 128
STEPS = 4
CHUNK = 128
UNIT = 256
MESH = pl.DeviceIdType.MESH
VMEM = pl.BlockSpec(memory_space=pltpu.VMEM)
SMEM = pl.BlockSpec(memory_space=pltpu.SMEM)
ANY = pl.BlockSpec(memory_space=pl.ANY)
NT = (((1,), (1,)), ((), ()))
BF = jnp.bfloat16
F32 = jnp.float32


def remote(src, dst, send, recv, device):
    return pltpu.make_async_remote_copy(
        src_ref=src, dst_ref=dst, send_sem=send, recv_sem=recv, device_id=device, device_id_type=MESH
    )


def others(axis_size, me):
    return [lax.rem(me + step, axis_size) for step in range(1, axis_size)]


def dot(a, b):
    return jnp.dot(a, b, preferred_element_type=F32)


def dot_nt(a, b):
    return lax.dot_general(a, b, NT, preferred_element_type=F32)


def norm_rows(values, gain):
    wide = values.astype(F32)
    factor = lax.rsqrt(jnp.mean(wide * wide, axis=-1, keepdims=True) + EPSILON)
    return (wide * factor * gain).astype(BF)


def renorm(updated, initial, axis):
    target_norm = jnp.sqrt(jnp.sum(initial * initial, axis=axis, keepdims=True))
    return (
        updated
        * target_norm
        * lax.rsqrt(jnp.sum(updated * updated, axis=axis, keepdims=True) + EPSILON)
    )


def layout(n, nh, slots, model, width, hidden):
    vmem, dma = pltpu.VMEM, pltpu.SemaphoreType.DMA
    part = PAIR // nh
    rows = part // STEPS
    wide = LANES * (-(-width // LANES))
    tokens = nh * PAIR
    parts = hidden // LANES
    chunk = 8 * (-(-3 * width // (8 * n)))
    outer = n // 2
    sizes = {}
    for c in range(STEPS):
        sizes[f"held{c}"] = vmem((slots, rows, model), BF)
        sizes[f"out{c}"] = vmem((n, rows, model), BF)
        sizes[f"in{c}"] = vmem((n, rows, model), BF)
        sizes[f"chosen{c}"] = vmem((nh, rows, model), BF)
    sizes.update(
        meta=vmem((n, 1, LANES), jnp.int32), meta_in=vmem((n, 1, LANES), jnp.int32),
        codes=pltpu.SMEM((n, 1, LANES), jnp.int32),
        w=vmem((4, nh, width, model), BF),
        pair=vmem((2, STEPS, nh // 2, rows, model), BF),
        q=vmem((PAIR, model), BF), k=vmem((PAIR, model), BF), v=vmem((PAIR, model), BF),
        a=vmem((CHUNK, model), BF), emb=vmem((nh, PAIR, model), BF),
        wf_in=vmem((3, width, model), BF), wr_in=vmem((1, model), BF),
        gu=vmem((2, width, hidden), F32), dt=vmem((width, hidden), F32),
        wf=vmem((3 * wide, model), BF), fq=vmem((tokens, wide), BF), fk=vmem((tokens, wide), BF),
        fkt=vmem((wide, tokens), BF), og=vmem((tokens, wide), BF), ogt=vmem((wide, tokens), BF),
        col=vmem((tokens, width), BF), two=vmem((tokens, 2 * LANES), BF), hk=vmem((tokens, LANES), BF),
        guw=vmem((parts, wide, 2 * LANES), BF), dth=vmem((wide, hidden), BF),
        g=vmem((max(3 * width, chunk * n), LANES), F32),
        total=vmem((max(3 * width, chunk * n), hidden), F32),
        ag=vmem((wide, 2 * hidden), BF), ad=vmem((width, hidden), BF),
        part=vmem((parts, 2, outer, chunk, LANES), BF), xin=vmem((parts, outer, chunk, LANES), BF),
        half=vmem((parts, outer, chunk, LANES), BF), zin=vmem((parts, outer - 1, chunk, LANES), BF),
        res=vmem((parts, 2, outer, chunk, LANES), BF),
        local=dma((STEPS + 7,)),
        xs=dma((STEPS, n - 1)), xr=dma((STEPS, n - 1)), ms=dma((n - 1,)), mr=dma((n - 1,)),
        ws=dma((3, 4)), wr=dma((3, 4)), ss=dma((STEPS, nh - 1)), sr=dma((STEPS, nh - 1)),
        gs=dma((3, PAIR // CHUNK)), gr=dma((3, PAIR // CHUNK)),
        ps=dma((parts,)), pr=dma((parts,)), zs=dma((parts, outer - 1)), zr=dma((parts, outer - 1)),
        rs=dma((parts, outer)), rr=dma((parts, outer)),
        fs=dma((parts, outer - 1)), fr=dma((parts, outer - 1)),
    )
    return sizes


def gradient_sum(n, width, s, side, lane, compute, during):
    seq = lax.axis_index("seq")
    outer_count = n // 2
    inner, outer = lax.rem(seq, 2), lax.div(seq, 2)
    parts = s.part.shape[0]
    chunk = s.part.shape[3]
    steps = range(1, outer_count)

    def plan(part):
        mine = s.res.at[part, inner, outer]
        theirs = [s.res.at[part, inner, lax.rem(outer + outer_count - t, outer_count)] for t in steps]
        return types.SimpleNamespace(
            x=remote(s.part.at[part, 1 - inner], s.xin.at[part], s.ps.at[part], s.pr.at[part], side),
            z=[
                remote(
                    s.half.at[part, lax.rem(outer + t, outer_count)], s.zin.at[part, t - 1],
                    s.zs.at[part, t - 1], s.zr.at[part, t - 1], lane[t - 1],
                )
                for t in steps
            ],
            r=[
                remote(mine, mine, s.rs.at[part, t], s.rr.at[part, t], to)
                for t, to in enumerate(lane + [side])
            ],
            f=[
                remote(theirs[t - 1], theirs[t - 1], s.fs.at[part, t - 1], s.fr.at[part, t - 1], side)
                for t in steps
            ],
        )

    plans = [plan(part) for part in range(parts)]

    def stage_x(part):
        plans[part].x.start()

    def stage_z(part):
        plans[part].x.wait_recv()
        for o in range(outer_count):
            s.half[part, o] = (
                s.part[part, inner, o].astype(F32) + s.xin[part, o].astype(F32)
            ).astype(BF)
        for copy in plans[part].z:
            copy.start()

    def stage_r(part):
        total = s.half[part, outer].astype(F32)
        for t, copy in enumerate(plans[part].z):
            copy.wait_recv()
            total = total + s.zin[part, t].astype(F32)
        s.res[part, inner, outer] = total.astype(BF)
        for copy in plans[part].r:
            copy.start()

    def stage_f(part):
        for t in steps:
            plans[part].r[t - 1].wait_recv()
            plans[part].f[t - 1].start()

    stages = [stage_x, stage_z, stage_r, stage_f]
    for tick in range(parts + len(stages) - 1):
        if tick < parts:
            compute(tick)
        for which, stage in enumerate(stages):
            if 0 <= tick - which < parts:
                stage(tick - which)
        if tick == parts - 1:
            during()
    for part in range(parts):
        plans[part].r[-1].wait_recv()
        for copy in plans[part].f:
            copy.wait_recv()
        cut = slice(part * LANES, (part + 1) * LANES)
        for i in range(2):
            for o in range(outer_count):
                at = (i * outer_count + o) * chunk
                s.total[at : at + chunk, cut] = s.res[part, i, o].astype(F32)
    for part in range(parts):
        plans[part].x.wait_send()
        for copy in plans[part].z + plans[part].r + plans[part].f:
            copy.wait_send()


def whole_kernel(
    n, nh, names, dest_ref, image_ref, x_ref, wqkv_ref, wo_ref, eg_ref, fg_ref, wf_ref, wr_ref,
    gu_ref, dt_ref, o_ref, *scratch,
):
    s = types.SimpleNamespace(**dict(zip(names, scratch)))
    seq, head = lax.axis_index("seq"), lax.axis_index("head")
    partner = head + 1 - 2 * lax.rem(head, 2)
    peer = lax.rem(head + nh // 2, nh)
    targets = others(n, seq)
    mates = others(nh, head)
    outer_count = n // 2
    inner, outer = lax.rem(seq, 2), lax.div(seq, 2)
    side = (outer * 2 + 1 - inner, head)
    lane = [(lax.rem(outer + t, outer_count) * 2 + inner, head) for t in range(1, outer_count)]
    model = x_ref.shape[-1]
    width, hidden = gu_ref.shape[1:]
    wide = s.fk.shape[1]
    parts = hidden // LANES
    tokens = nh * PAIR
    held = [getattr(s, f"held{c}") for c in range(STEPS)]
    out = [getattr(s, f"out{c}") for c in range(STEPS)]
    arrived = [getattr(s, f"in{c}") for c in range(STEPS)]
    chosen = [getattr(s, f"chosen{c}") for c in range(STEPS)]
    rows = held[0].shape[1]
    per_block = nh // 2

    barrier = pltpu.get_barrier_semaphore()
    greeted = [(to, head) for to in targets] + [(seq, to) for to in mates]
    for device in greeted:
        pl.semaphore_signal(barrier, inc=1, device_id=device, device_id_type=MESH)

    fetch = [
        pltpu.make_async_copy(x_ref.at[:, lax.rem(head, per_block), c], held[c], s.local.at[c])
        for c in range(STEPS)
    ]
    weights_in = [
        pltpu.make_async_copy(wqkv_ref, s.w.at[0:3, head], s.local.at[STEPS]),
        pltpu.make_async_copy(wo_ref, s.w.at[3, head], s.local.at[STEPS + 1]),
    ]
    late = [
        pltpu.make_async_copy(src, dst, s.local.at[STEPS + 2 + which])
        for which, (src, dst) in enumerate(
            [(wf_ref, s.wf_in), (wr_ref, s.wr_in), (gu_ref, s.gu), (dt_ref, s.dt)]
        )
    ]
    for copy in fetch[:1] + weights_in + fetch[1:] + late:
        copy.start()

    my_block = lax.div(head, per_block)
    pairs = dest_ref.shape[0] // 2
    firsts = [dest_ref[2 * i] for i in range(pairs)]
    sames = [(image_ref[2 * i] == image_ref[2 * i + 1]).astype(jnp.int32) for i in range(pairs)]
    homes = [lax.div(jnp.maximum(d, 0), BLK_DEV) for d in firsts]
    slots = []
    for i, d in enumerate(firsts):
        slots.append(2 * i + lax.rem(jnp.maximum(d, 0) + my_block, 2))
    marks = [
        2 * lax.div(lax.rem(jnp.maximum(d, 0), BLK_DEV), 2) + same for d, same in zip(firsts, sames)
    ]

    def lookup(target):
        slot, code = jnp.int32(0), jnp.int32(-1)
        for i, d in enumerate(firsts):
            hit = jnp.logical_and(d >= 0, homes[i] == target)
            slot = jnp.where(hit, slots[i], slot)
            code = jnp.where(hit, marks[i], code)
        return slot, code

    found = [lookup(to) for to in targets + [seq]]
    for step, to in enumerate(targets):
        s.meta[step] = jnp.full((1, LANES), found[step][1], jnp.int32)
    s.meta_in[seq] = jnp.full((1, LANES), found[-1][1], jnp.int32)

    def pick(c):
        fetch[c].wait()
        for step in range(n - 1):
            out[c][step] = held[c][found[step][0]]
        arrived[c][seq] = held[c][found[-1][0]]

    meta_copies = [
        remote(s.meta.at[step], s.meta_in.at[seq], s.ms.at[step], s.mr.at[step], (to, head))
        for step, to in enumerate(targets)
    ]
    x_copies = [
        [
            remote(out[c].at[step], arrived[c].at[seq], s.xs.at[c, step], s.xr.at[c, step], (to, head))
            for step, to in enumerate(targets)
        ]
        for c in range(STEPS)
    ]
    to_peer = [
        remote(s.w.at[m, head], s.w.at[m, head], s.ws.at[0, m], s.wr.at[0, m], (seq, peer))
        for m in range(4)
    ]
    to_partner = [
        remote(s.w.at[m, head], s.w.at[m, head], s.ws.at[1, m], s.wr.at[1, m], (seq, partner))
        for m in range(4)
    ]
    passed = [
        remote(s.w.at[m, peer], s.w.at[m, peer], s.ws.at[2, m], s.wr.at[2, m], (seq, partner))
        for m in range(4)
    ]
    pick(0)
    pl.semaphore_wait(barrier, len(greeted))
    for copy in meta_copies + x_copies[0]:
        copy.start()
    for copy in weights_in:
        copy.wait()
    for copy in to_peer + to_partner:
        copy.start()
    for c in range(1, STEPS):
        pick(c)
        for copy in x_copies[c]:
            copy.start()

    s.wf[...] = jnp.zeros_like(s.wf)
    s.guw[...] = jnp.zeros_like(s.guw)
    s.dth[...] = jnp.zeros_like(s.dth)
    s.g[...] = jnp.zeros_like(s.g)
    s.ag[...] = jnp.zeros_like(s.ag)
    for copy in late:
        copy.wait()
    for which in range(3):
        s.wf[which * wide : which * wide + width] = s.wf_in[which]
    rate_at = 2 * wide + width
    s.wf[rate_at : rate_at + 16] = jnp.broadcast_to(s.wr_in[...], (16, model))
    s.dth[:width] = s.dt[...].astype(BF)
    for part in range(parts):
        cut = slice(part * LANES, (part + 1) * LANES)
        s.guw[part, :width, :LANES] = s.gu[0, :, cut].astype(BF)
        s.guw[part, :width, LANES:] = s.gu[1, :, cut].astype(BF)

    for copy in meta_copies:
        copy.wait_recv()
    spread = pltpu.make_async_copy(s.meta_in, s.codes, s.local.at[STEPS + 6])
    spread.start()
    spread.wait()
    sources = [jnp.int32(0)] * nh
    same = jnp.int32(0)
    for source in range(n):
        code = s.codes[source, 0, 0]
        place = lax.div(jnp.maximum(code, 0), 2)
        for p in range(nh):
            sources[p] = jnp.where(jnp.logical_and(code >= 0, place == p), source, sources[p])
        mine = jnp.logical_and(code >= 0, place == head)
        same = jnp.where(mine, lax.rem(jnp.maximum(code, 0), 2), same)

    swaps = [
        [
            remote(
                chosen[c].at[to], s.pair.at[lax.div(head, per_block), c, lax.rem(head, per_block)],
                s.ss.at[c, step], s.sr.at[c, step], (seq, to),
            )
            for step, to in enumerate(mates)
        ]
        for c in range(STEPS)
    ]

    def swap(c):
        for copy in x_copies[c]:
            copy.wait_recv()
        for p in range(nh):
            chosen[c][p] = arrived[c][sources[p]]
        for copy in swaps[c]:
            copy.start()
        s.pair[lax.div(head, per_block), c, lax.rem(head, per_block)] = chosen[c][head]

    def matrix(m):
        return s.w[m].reshape(nh * width, model)

    run = per_block * rows

    def project(c):
        for copy in swaps[c]:
            copy.wait_recv()
        taken = jnp.concatenate([s.pair[b, c].reshape(run, model) for b in range(2)], axis=0)
        normed = norm_rows(taken, eg_ref[...])
        for m, ref in enumerate((s.q, s.k, s.v)):
            value = dot_nt(normed, matrix(m)).astype(BF)
            if m == 0:
                value = value * BF(HDIM ** (-0.5))
            for b in range(2):
                at = b * BLK + c * run
                ref[at : at + run] = value[b * run : (b + 1) * run]

    def forward(m):
        to_peer[m].wait_recv()
        passed[m].start()

    for c in range(STEPS):
        swap(c)
        if c == STEPS - 2:
            for m in range(4):
                forward(m)
            for m in range(3):
                to_partner[m].wait_recv()
                passed[m].wait_recv()
            for early in range(c):
                project(early)
    project(STEPS - 2)
    project(STEPS - 1)
    to_partner[3].wait_recv()
    passed[3].wait_recv()

    apart = jnp.where(same > 0, 0.0, -1e30).astype(F32)
    key_block = lax.broadcasted_iota(jnp.int32, (1, PAIR), 1) // BLK
    first = lax.broadcasted_iota(jnp.int32, (CHUNK, LANES), 1) < HDIM
    chunks = PAIR // CHUNK

    def emb_copies(i):
        at = pl.ds(i * CHUNK, CHUNK)
        mine, theirs = s.emb.at[head, at], s.emb.at[peer, at]
        return [
            remote(mine, mine, s.gs.at[0, i], s.gr.at[0, i], (seq, peer)),
            remote(mine, mine, s.gs.at[1, i], s.gr.at[1, i], (seq, partner)),
            remote(theirs, theirs, s.gs.at[2, i], s.gr.at[2, i], (seq, partner)),
        ]

    gathers = [emb_copies(i) for i in range(chunks)]

    def attend(i):
        at = pl.ds(i * CHUNK, CHUNK)
        bias = jnp.where(key_block == i * CHUNK // BLK, 0.0, apart)

        def slabs(index, carry):
            for half in range(2):
                columns = pl.ds(pl.multiple_of((2 * index + half) * LANES, LANES), LANES)
                query = s.q[at, columns]
                nothing = jnp.zeros_like(query)
                both = jnp.concatenate(
                    [jnp.where(first, query, nothing), jnp.where(first, nothing, query)], axis=0
                )
                scores = dot_nt(both, s.k[:, columns]) + bias
                top = jnp.max(scores, axis=-1, keepdims=True)
                weights = jnp.exp(scores - top)
                total = jnp.sum(weights, axis=-1, keepdims=True)
                mixed = dot(weights.astype(BF), s.v[:, columns]) * (1.0 / total)
                s.a[:, columns] = jnp.where(first, mixed[:CHUNK], mixed[CHUNK:]).astype(BF)
            return carry

        lax.fori_loop(0, model // LANES // 2, slabs, 0)
        mixed = dot(s.a[...], matrix(3))
        taken = s.pair[i * CHUNK // BLK].reshape(BLK, model)
        low = i * CHUNK % BLK
        s.emb[head, at] = (taken[low : low + CHUNK].astype(F32) + mixed).astype(BF)
        gathers[i][0].start()
        gathers[i][1].start()

    scale = RATE_SCALE * (tokens * n) ** (-0.5)

    def fast_project(owner, i):
        at = pl.ds(pl.multiple_of(owner * PAIR + i * CHUNK, CHUNK), CHUNK)
        normed = norm_rows(s.emb[owner, pl.ds(i * CHUNK, CHUNK)], fg_ref[...])
        mapped = dot_nt(normed, s.wf[...])
        s.fq[at] = mapped[:, :wide].astype(BF)
        key = mapped[:, wide : 2 * wide].astype(BF)
        s.fk[at] = key
        s.fkt[:, at] = key.T
        value = mapped[:, 2 * wide :].astype(BF).astype(F32)
        before = mapped[:, rate_at : rate_at + 1]
        soft = jnp.maximum(before, 0.0) + jnp.log1p(jnp.exp(-jnp.abs(before)))
        back = (-(scale * soft) * value).astype(BF)
        s.og[at] = back
        s.ogt[:, at] = back.T

    for i in range(chunks):
        attend(i)
        fast_project(head, i)
        if i >= 1:
            gathers[i - 1][0].wait_recv()
            gathers[i - 1][2].start()
    across = lax.rem(partner + nh // 2, nh)
    for i in range(chunks):
        if i == chunks - 1:
            gathers[i][0].wait_recv()
            gathers[i][2].start()
        gathers[i][1].wait_recv()
        fast_project(partner, i)
        fast_project(peer, i)
        gathers[i][2].wait_recv()
        fast_project(across, i)

    def compute(part):
        def body(unit, carry):
            at = pl.ds(pl.multiple_of(unit * UNIT, UNIT), UNIT)
            both = dot(s.fk[at], s.guw[part])
            gate, up = both[:, :LANES], both[:, LANES:]
            grad = dot(s.og[at], s.dth[:, part * LANES : (part + 1) * LANES])
            sig = jax.nn.sigmoid(gate)
            silu = gate * sig
            s.hk[at] = (silu * up).astype(BF)
            s.two[at, :LANES] = (grad * up * sig * (1.0 + gate * (1.0 - sig))).astype(BF)
            s.two[at, LANES:] = (grad * silu).astype(BF)
            return carry

        lax.fori_loop(0, tokens // UNIT, body, 0)
        one = dot(s.fkt[...], s.two[...])
        other = dot(s.ogt[...], s.hk[...])
        s.g[0:width] = one[:width, :LANES]
        s.g[width : 2 * width] = one[:width, LANES:]
        s.g[2 * width : 3 * width] = other[:width]
        chunk = s.part.shape[3]
        for i in range(2):
            for o in range(outer_count):
                at = (i * outer_count + o) * chunk
                s.part[part, i, o] = s.g[at : at + chunk].astype(BF)

    def during():
        for which in range(model // width):

            @pl.when(head == which)
            def _():
                for owner in range(nh):
                    at = owner * PAIR
                    s.col[at : at + PAIR] = s.emb[owner, :, which * width : (which + 1) * width]

    gradient_sum(n, width, s, side, lane, compute, during)

    for which in range(2):
        start = s.gu[which]
        fresh = renorm(start - s.total[which * width : (which + 1) * width], start, 1)
        s.ag[:width, which * hidden : (which + 1) * hidden] = fresh.astype(BF)
    start = s.dt[...]
    s.ad[...] = renorm(start - s.total[2 * width : 3 * width], start, 0).astype(BF)

    def final(unit, carry):
        base = pl.multiple_of(unit * BLK, BLK)
        at = pl.ds(base, BLK)
        both = dot(s.fq[at], s.ag[...])
        gate = both[:, :hidden]
        inside = (gate * jax.nn.sigmoid(gate) * both[:, hidden:]).astype(BF)
        done = (s.col[at].astype(F32) + dot_nt(inside, s.ad[...])).astype(BF)
        for c in range(STEPS):
            for which in range(per_block):
                low = (c * per_block + which) * rows
                to = pl.multiple_of(base + which * STEPS * rows + c * rows, rows)
                o_ref[pl.ds(to, rows)] = done[low : low + rows]
        return carry

    lax.fori_loop(0, tokens // BLK, final, 0)

    for copy in meta_copies + to_peer + to_partner + passed:
        copy.wait_send()
    for group in x_copies + swaps + gathers:
        for copy in group:
            copy.wait_send()


def on_device(
    patches,
    slot_image,
    slot_dest,
    enc_gain,
    w_qkv,
    w_out,
    fast_gain,
    w_fast,
    w_rate,
    fast_gate_up,
    fast_down,
):
    n = lax.axis_size("seq")
    nh = lax.axis_size("head")
    model = patches.shape[1]
    slots = slot_dest.shape[0]
    width, hidden = fast_gate_up.shape[2:]
    part = PAIR // nh
    sizes = layout(n, nh, slots, model, width, hidden)
    return pl.pallas_call(
        functools.partial(whole_kernel, n, nh, tuple(sizes)),
        out_shape=jax.ShapeDtypeStruct((nh * PAIR, width), patches.dtype),
        in_specs=[SMEM, SMEM, ANY, ANY, ANY, VMEM, VMEM, ANY, ANY, ANY, ANY],
        out_specs=VMEM,
        scratch_shapes=list(sizes.values()),
        compiler_params=pltpu.CompilerParams(
            collective_id=1, has_side_effects=True, vmem_limit_bytes=60 * 1024 * 1024
        ),
        name="encode_and_update",
    )(
        slot_dest,
        slot_image,
        patches.reshape(slots, BLK // part, STEPS, part // STEPS, model),
        jnp.swapaxes(w_qkv, 1, 2),
        w_out,
        enc_gain[None, :],
        fast_gain[None, :],
        jnp.swapaxes(w_fast, 1, 2),
        w_rate.T,
        fast_gate_up[0],
        fast_down[0].T,
    )


def solution(mesh):
    in_specs = (
        P("seq", None),
        P("seq"),
        P("seq"),
        P(),
        P(None, None, "head"),
        P("head", None),
        P(),
        P(None, None, "head"),
        P(None, "head"),
        P("head", None, None, None),
        P("head", None, None),
    )
    out_specs = P("seq", "head")
    return jax.shard_map(
        on_device, mesh=mesh, in_specs=in_specs, out_specs=out_specs, check_vma=False
    )
```

time: 156 us -> 109 us (0.70); the launches traced: 153 us -> 109 us
  matrix products: 17.2 us -> 0 us
  Pallas kernels: 119 us -> 104 us
  other arithmetic: 7.2 us -> 0 us
  local copies, waits for them, and re-layouts: 9.67 us -> 4.73 us
    dot_general x12 -> x0, matrix products: 17.2 us -> none  [the longest x1 4.34 us: on_device(): jnp.dot(query_hidden, applied_down.T, preferred_element_type=jnp.float32)]
    pallas_call x6 -> x1, Pallas kernels: 119 us -> 104 us  [on_device(): pl.pallas_call(functools.partial(whole_kernel, n, nh, tuple(sizes)), out_...]
    unnamed x19 -> x0, local copies, waits for them, and re-layouts: 4.77 us -> none
    concatenate x3 -> x0, other arithmetic: 3.34 us -> none  [the longest x1 2.49 us: on_device(): weights = jnp.concatenate([jnp.swapaxes(w_qkv, 1, 2), w_out[None]], axis=0)]
    reduce_sum x2 -> x0, other arithmetic: 2.97 us -> none  [the longest x1 2.73 us: norm_rows(): jnp.mean(widened * widened, axis=-1, keepdims=True) + EPSILON]
    pallas_call x0 -> x1, local copies, waits for them, and re-layouts: none -> 2.19 us  [on_device(): pl.pallas_call(functools.partial(whole_kernel, n, nh, tuple(sizes)), out_...]
    slice x3 -> x0, local copies, waits for them, and re-layouts: 2.15 us -> none  [the longest x1 1.08 us: from_tiles(): flat[c * rows:(c + 1) * rows]]
where the time goes in v2:
time: 109 us
  Pallas kernels  104 us (95%)
  local copies, waits for them, and re-layouts  4.73 us (4%)
    pallas_call x1, Pallas kernels, on_device(): pl.pallas_call(functools.partial(whole_kernel, n, nh, tuple(sizes)), out_...  104 us
    pallas_call x1, local copies, waits for them, and re-layouts, on_device(): pl.pallas_call(functools.partial(whole_kernel, n, nh, tuple(sizes)), out_...  2.19 us

profile of v2, /device:TPU:0, one launch (start us, length us, event | category | flops | bytes accessed | tf_op | source)
XLA Modules:
  0.0 109.1 jit_solution(2841488689882657325)
XLA Ops:
  0.0 1.3 %broadcast_in_dim.6.eg_ref = f32[1,768]{1,0:T(1,128)} reshape(f32[768]{0:T(1024)} %param.14) | data formatting | bytes 6144 | tf_op jit(solution)/shard_map/broadcast_in_dim | solution.py:574
  1.3 1.3 %broadcast_in_dim.7.fg_ref = f32[1,768]{1,0:T(1,128)} reshape(f32[768]{0:T(1024)} %param.17) | data formatting | bytes 6144 | tf_op jit(solution)/shard_map/broadcast_in_dim | solution.py:575
  2.5 104.3 %encode_and_update.1 = bf16[2048,192]{1,0:T(8,128)(2,1)} custom-call(s32[16]{0:T(128)} %dest_ref.1, s32[16]{0:T(128)} %image_ref.1, bf16[16,2,4,32,768]{4,3,2,1,0:T(8,128)(2,1)} %bitcast.8, bf16[3,192,768]{2,1,0:T(8,128)(2,1)} %bitcast.9, bf16[192,768]{1,0:T(8,128)(2,1)} %wo_ref.1, f32[1,768]{1,0:T(1,128)} %broadcast_in_dim.6.eg_ref, ...), custom_call_target="tpu_custom_call" | custom-call | tf_op jit(solution)/shard_map/encode_and_update/pallas_call | solution.py:558
  106.9 2.2 %copy.12 = bf16[2048,192]{0,1:T(8,128)(2,1)} copy(bf16[2048,192]{1,0:T(8,128)(2,1)} %encode_and_update.1) | data formatting | bytes 1572864 | tf_op jit(solution)/shard_map/encode_and_update/pallas_call | solution.py:558

commit v3 on v2

--- a/solution.py
+++ b/solution.py
@@ -94,7 +94,9 @@
         part=vmem((parts, 2, outer, chunk, LANES), BF), xin=vmem((parts, outer, chunk, LANES), BF),
         half=vmem((parts, outer, chunk, LANES), BF), zin=vmem((parts, outer - 1, chunk, LANES), BF),
         res=vmem((parts, 2, outer, chunk, LANES), BF),
-        local=dma((STEPS + 7,)),
+        eg_in=vmem((model // LANES, LANES), F32), fg_in=vmem((model // LANES, LANES), F32),
+        eg=vmem((1, model), F32), fg=vmem((1, model), F32), done=vmem((tokens, width), BF),
+        local=dma((STEPS + 9,)), put=dma((tokens // BLK,)),
         xs=dma((STEPS, n - 1)), xr=dma((STEPS, n - 1)), ms=dma((n - 1,)), mr=dma((n - 1,)),
         ws=dma((3, 4)), wr=dma((3, 4)), ss=dma((STEPS, nh - 1)), sr=dma((STEPS, nh - 1)),
         gs=dma((3, PAIR // CHUNK)), gr=dma((3, PAIR // CHUNK)),
@@ -232,7 +234,11 @@
             [(wf_ref, s.wf_in), (wr_ref, s.wr_in), (gu_ref, s.gu), (dt_ref, s.dt)]
         )
     ]
-    for copy in fetch[:1] + weights_in + fetch[1:] + late:
+    gains_in = [
+        pltpu.make_async_copy(src, dst, s.local.at[STEPS + 7 + which])
+        for which, (src, dst) in enumerate([(eg_ref, s.eg_in), (fg_ref, s.fg_in)])
+    ]
+    for copy in fetch[:1] + weights_in + fetch[1:] + late + gains_in:
         copy.start()
 
     my_block = lax.div(head, per_block)
@@ -307,8 +313,11 @@
     s.dth[...] = jnp.zeros_like(s.dth)
     s.g[...] = jnp.zeros_like(s.g)
     s.ag[...] = jnp.zeros_like(s.ag)
-    for copy in late:
+    for copy in late + gains_in:
         copy.wait()
+    for src, dst in ((s.eg_in, s.eg), (s.fg_in, s.fg)):
+        for which in range(model // LANES):
+            dst[:, which * LANES : (which + 1) * LANES] = src[which : which + 1]
     for which in range(3):
         s.wf[which * wide : which * wide + width] = s.wf_in[which]
     rate_at = 2 * wide + width
@@ -363,7 +372,7 @@
         for copy in swaps[c]:
             copy.wait_recv()
         taken = jnp.concatenate([s.pair[b, c].reshape(run, model) for b in range(2)], axis=0)
-        normed = norm_rows(taken, eg_ref[...])
+        normed = norm_rows(taken, s.eg[...])
         for m, ref in enumerate((s.q, s.k, s.v)):
             value = dot_nt(normed, matrix(m)).astype(BF)
             if m == 0:
@@ -439,7 +448,7 @@
 
     def fast_project(owner, i):
         at = pl.ds(pl.multiple_of(owner * PAIR + i * CHUNK, CHUNK), CHUNK)
-        normed = norm_rows(s.emb[owner, pl.ds(i * CHUNK, CHUNK)], fg_ref[...])
+        normed = norm_rows(s.emb[owner, pl.ds(i * CHUNK, CHUNK)], s.fg[...])
         mapped = dot_nt(normed, s.wf[...])
         s.fq[at] = mapped[:, :wide].astype(BF)
         key = mapped[:, wide : 2 * wide].astype(BF)
@@ -459,15 +468,20 @@
             gathers[i - 1][0].wait_recv()
             gathers[i - 1][2].start()
     across = lax.rem(partner + nh // 2, nh)
-    for i in range(chunks):
-        if i == chunks - 1:
-            gathers[i][0].wait_recv()
-            gathers[i][2].start()
+    for i in range(chunks - 1):
         gathers[i][1].wait_recv()
         fast_project(partner, i)
         fast_project(peer, i)
+    gathers[chunks - 1][1].wait_recv()
+    fast_project(partner, chunks - 1)
+    for i in range(chunks - 1):
         gathers[i][2].wait_recv()
         fast_project(across, i)
+    gathers[chunks - 1][0].wait_recv()
+    gathers[chunks - 1][2].start()
+    fast_project(peer, chunks - 1)
+    gathers[chunks - 1][2].wait_recv()
+    fast_project(across, chunks - 1)
 
     def compute(part):
         def body(unit, carry):
@@ -482,7 +496,7 @@
             s.two[at, LANES:] = (grad * silu).astype(BF)
             return carry
 
-        lax.fori_loop(0, tokens // UNIT, body, 0)
+        lax.fori_loop(0, tokens // UNIT, body, 0, unroll=2)
         one = dot(s.fkt[...], s.two[...])
         other = dot(s.ogt[...], s.hk[...])
         s.g[0:width] = one[:width, :LANES]
@@ -511,6 +525,10 @@
         s.ag[:width, which * hidden : (which + 1) * hidden] = fresh.astype(BF)
     start = s.dt[...]
     s.ad[...] = renorm(start - s.total[2 * width : 3 * width], start, 0).astype(BF)
+
+    def put(unit):
+        at = pl.ds(unit * BLK, BLK)
+        return pltpu.make_async_copy(s.done.at[at], o_ref.at[at], s.put.at[unit])
 
     def final(unit, carry):
         base = pl.multiple_of(unit * BLK, BLK)
@@ -523,10 +541,13 @@
             for which in range(per_block):
                 low = (c * per_block + which) * rows
                 to = pl.multiple_of(base + which * STEPS * rows + c * rows, rows)
-                o_ref[pl.ds(to, rows)] = done[low : low + rows]
+                s.done[pl.ds(to, rows)] = done[low : low + rows]
+        put(unit).start()
         return carry
 
-    lax.fori_loop(0, tokens // BLK, final, 0)
+    lax.fori_loop(0, tokens // BLK, final, 0, unroll=2)
+    for unit in range(tokens // BLK):
+        put(unit).wait()
 
     for copy in meta_copies + to_peer + to_partner + passed:
         copy.wait_send()
@@ -558,8 +579,8 @@
     return pl.pallas_call(
         functools.partial(whole_kernel, n, nh, tuple(sizes)),
         out_shape=jax.ShapeDtypeStruct((nh * PAIR, width), patches.dtype),
-        in_specs=[SMEM, SMEM, ANY, ANY, ANY, VMEM, VMEM, ANY, ANY, ANY, ANY],
-        out_specs=VMEM,
+        in_specs=[SMEM, SMEM] + [ANY] * 9,
+        out_specs=ANY,
         scratch_shapes=list(sizes.values()),
         compiler_params=pltpu.CompilerParams(
             collective_id=1, has_side_effects=True, vmem_limit_bytes=60 * 1024 * 1024
@@ -571,8 +592,8 @@
         patches.reshape(slots, BLK // part, STEPS, part // STEPS, model),
         jnp.swapaxes(w_qkv, 1, 2),
         w_out,
-        enc_gain[None, :],
-        fast_gain[None, :],
+        enc_gain.reshape(model // LANES, LANES),
+        fast_gain.reshape(model // LANES, LANES),
         jnp.swapaxes(w_fast, 1, 2),
         w_rate.T,
         fast_gate_up[0],

time: 109 us -> 106 us (0.972)
  local copies, waits for them, and re-layouts: 4.73 us -> 2.19 us
    broadcast_in_dim x2 -> x0, local copies, waits for them, and re-layouts: 2.54 us -> none  [the longest x1 1.28 us: on_device(): fast_gain[None, :]]
where the time goes in v3:
time: 106 us
  Pallas kernels  103 us (97%)
  local copies, waits for them, and re-layouts  2.19 us (2%)
    pallas_call x1, Pallas kernels, on_device(): pl.pallas_call(functools.partial(whole_kernel, n, nh, tuple(sizes)), out_...  103 us
    pallas_call x1, local copies, waits for them, and re-layouts, on_device(): pl.pallas_call(functools.partial(whole_kernel, n, nh, tuple(sizes)), out_...  2.19 us

profile of v3, /device:TPU:0, one launch (start us, length us, event | category | flops | bytes accessed | tf_op | source)
XLA Modules:
  0.0 105.5 jit_solution(8006754184898767781)
XLA Ops:
  0.0 103.3 %encode_and_update.1 = bf16[2048,192]{1,0:T(8,128)(2,1)} custom-call(s32[16]{0:T(128)} %dest_ref.1, s32[16]{0:T(128)} %image_ref.1, bf16[16,2,4,32,768]{4,3,2,1,0:T(8,128)(2,1)} %bitcast.10, bf16[3,192,768]{2,1,0:T(8,128)(2,1)} %bitcast.11, bf16[192,768]{1,0:T(8,128)(2,1)} %wo_ref.1, f32[6,128]{1,0:T(8,128)} %bitcast.15, f32[6,128]{1,0:T(8,128)} %bitcast.16, ...), custom_call_target="tpu_custom_call" | custom-call | tf_op jit(solution)/shard_map/encode_and_update/pallas_call | solution.py:579
  103.4 2.2 %copy.12 = bf16[2048,192]{0,1:T(8,128)(2,1)} copy(bf16[2048,192]{1,0:T(8,128)(2,1)} %encode_and_update.1) | data formatting | bytes 1572864 | tf_op jit(solution)/shard_map/encode_and_update/pallas_call | solution.py:579

commit v4 on v3

--- a/solution.py
+++ b/solution.py
@@ -80,13 +80,14 @@
         codes=pltpu.SMEM((n, 1, LANES), jnp.int32),
         w=vmem((4, nh, width, model), BF),
         pair=vmem((2, STEPS, nh // 2, rows, model), BF),
-        q=vmem((PAIR, model), BF), k=vmem((PAIR, model), BF), v=vmem((PAIR, model), BF),
+        q=vmem((PAIR, model), BF), k=vmem((PAIR, model), BF), v=vmem((PAIR, 2 * model), BF),
         a=vmem((CHUNK, model), BF), emb=vmem((nh, PAIR, model), BF),
         wf_in=vmem((3, width, model), BF), wr_in=vmem((1, model), BF),
         gu=vmem((2, width, hidden), F32), dt=vmem((width, hidden), F32),
-        wf=vmem((3 * wide, model), BF), fq=vmem((tokens, wide), BF), fk=vmem((tokens, wide), BF),
-        fkt=vmem((wide, tokens), BF), og=vmem((tokens, wide), BF), ogt=vmem((wide, tokens), BF),
-        col=vmem((tokens, width), BF), two=vmem((tokens, 2 * LANES), BF), hk=vmem((tokens, LANES), BF),
+        wf=vmem((3 * wide, model), BF), fq=vmem((tokens, wide), BF),
+        fkt=vmem((wide, tokens), BF), ogt=vmem((wide, tokens), BF),
+        col=vmem((tokens, width), BF), two=vmem((parts, tokens, 2 * LANES), BF),
+        hk=vmem((parts, tokens, LANES), BF),
         guw=vmem((parts, wide, 2 * LANES), BF), dth=vmem((wide, hidden), BF),
         g=vmem((max(3 * width, chunk * n), LANES), F32),
         total=vmem((max(3 * width, chunk * n), hidden), F32),
@@ -205,7 +206,7 @@
     lane = [(lax.rem(outer + t, outer_count) * 2 + inner, head) for t in range(1, outer_count)]
     model = x_ref.shape[-1]
     width, hidden = gu_ref.shape[1:]
-    wide = s.fk.shape[1]
+    wide = s.fq.shape[1]
     parts = hidden // LANES
     tokens = nh * PAIR
     held = [getattr(s, f"held{c}") for c in range(STEPS)]
@@ -309,6 +310,7 @@
             copy.start()
 
     s.wf[...] = jnp.zeros_like(s.wf)
+    s.v[...] = jnp.ones_like(s.v)
     s.guw[...] = jnp.zeros_like(s.guw)
     s.dth[...] = jnp.zeros_like(s.dth)
     s.g[...] = jnp.zeros_like(s.g)
@@ -373,13 +375,16 @@
             copy.wait_recv()
         taken = jnp.concatenate([s.pair[b, c].reshape(run, model) for b in range(2)], axis=0)
         normed = norm_rows(taken, s.eg[...])
-        for m, ref in enumerate((s.q, s.k, s.v)):
-            value = dot_nt(normed, matrix(m)).astype(BF)
-            if m == 0:
-                value = value * BF(HDIM ** (-0.5))
-            for b in range(2):
-                at = b * BLK + c * run
-                ref[at : at + run] = value[b * run : (b + 1) * run]
+        values = [dot_nt(normed, matrix(m)).astype(BF) for m in range(3)]
+        values[0] = values[0] * BF(HDIM ** (-0.5))
+        for b in range(2):
+            at = b * BLK + c * run
+            s.q[at : at + run] = values[0][b * run : (b + 1) * run]
+            s.k[at : at + run] = values[1][b * run : (b + 1) * run]
+            for slab in range(model // LANES):
+                s.v[at : at + run, 2 * slab * LANES : (2 * slab + 1) * LANES] = values[2][
+                    b * run : (b + 1) * run, slab * LANES : (slab + 1) * LANES
+                ]
 
     def forward(m):
         to_peer[m].wait_recv()
@@ -406,43 +411,37 @@
     chunks = PAIR // CHUNK
 
     def emb_copies(i):
-        at = pl.ds(i * CHUNK, CHUNK)
+        at = pl.ds(pl.multiple_of(i * CHUNK, CHUNK), CHUNK)
         mine, theirs = s.emb.at[head, at], s.emb.at[peer, at]
-        return [
-            remote(mine, mine, s.gs.at[0, i], s.gr.at[0, i], (seq, peer)),
-            remote(mine, mine, s.gs.at[1, i], s.gr.at[1, i], (seq, partner)),
-            remote(theirs, theirs, s.gs.at[2, i], s.gr.at[2, i], (seq, partner)),
-        ]
-
-    gathers = [emb_copies(i) for i in range(chunks)]
+        return types.SimpleNamespace(
+            peer=remote(mine, mine, s.gs.at[0, i], s.gr.at[0, i], (seq, peer)),
+            partner=remote(mine, mine, s.gs.at[1, i], s.gr.at[1, i], (seq, partner)),
+            across=remote(theirs, theirs, s.gs.at[2, i], s.gr.at[2, i], (seq, partner)),
+        )
+
+    per_chunk = CHUNK // run
 
     def attend(i):
-        at = pl.ds(i * CHUNK, CHUNK)
-        bias = jnp.where(key_block == i * CHUNK // BLK, 0.0, apart)
-
-        def slabs(index, carry):
-            for half in range(2):
-                columns = pl.ds(pl.multiple_of((2 * index + half) * LANES, LANES), LANES)
-                query = s.q[at, columns]
-                nothing = jnp.zeros_like(query)
-                both = jnp.concatenate(
-                    [jnp.where(first, query, nothing), jnp.where(first, nothing, query)], axis=0
-                )
-                scores = dot_nt(both, s.k[:, columns]) + bias
-                top = jnp.max(scores, axis=-1, keepdims=True)
-                weights = jnp.exp(scores - top)
-                total = jnp.sum(weights, axis=-1, keepdims=True)
-                mixed = dot(weights.astype(BF), s.v[:, columns]) * (1.0 / total)
-                s.a[:, columns] = jnp.where(first, mixed[:CHUNK], mixed[CHUNK:]).astype(BF)
-            return carry
-
-        lax.fori_loop(0, model // LANES // 2, slabs, 0)
+        at = pl.ds(pl.multiple_of(i * CHUNK, CHUNK), CHUNK)
+        block = lax.div(i, BLK // CHUNK)
+        bias = jnp.where(key_block == block, 0.0, apart)
+        for slab in range(model // LANES):
+            columns = slice(slab * LANES, (slab + 1) * LANES)
+            query = s.q[at, columns]
+            nothing = jnp.zeros_like(query)
+            both = jnp.concatenate(
+                [jnp.where(first, query, nothing), jnp.where(first, nothing, query)], axis=0
+            )
+            scores = dot_nt(both, s.k[:, columns]) + bias
+            top = jnp.max(scores, axis=-1, keepdims=True)
+            weights = jnp.exp(scores - top).astype(BF)
+            mixed = dot(weights, s.v[:, 2 * slab * LANES : 2 * (slab + 1) * LANES])
+            mixed = mixed[:, :LANES] * (1.0 / mixed[:, LANES:])
+            s.a[:, columns] = jnp.where(first, mixed[:CHUNK], mixed[CHUNK:]).astype(BF)
         mixed = dot(s.a[...], matrix(3))
-        taken = s.pair[i * CHUNK // BLK].reshape(BLK, model)
-        low = i * CHUNK % BLK
-        s.emb[head, at] = (taken[low : low + CHUNK].astype(F32) + mixed).astype(BF)
-        gathers[i][0].start()
-        gathers[i][1].start()
+        low = lax.rem(i, BLK // CHUNK) * per_chunk
+        taken = s.pair[block, pl.ds(low, per_chunk)].reshape(CHUNK, model)
+        s.emb[head, at] = (taken.astype(F32) + mixed).astype(BF)
 
     scale = RATE_SCALE * (tokens * n) ** (-0.5)
 
@@ -452,53 +451,65 @@
         mapped = dot_nt(normed, s.wf[...])
         s.fq[at] = mapped[:, :wide].astype(BF)
         key = mapped[:, wide : 2 * wide].astype(BF)
-        s.fk[at] = key
         s.fkt[:, at] = key.T
         value = mapped[:, 2 * wide :].astype(BF).astype(F32)
         before = mapped[:, rate_at : rate_at + 1]
         soft = jnp.maximum(before, 0.0) + jnp.log1p(jnp.exp(-jnp.abs(before)))
         back = (-(scale * soft) * value).astype(BF)
-        s.og[at] = back
         s.ogt[:, at] = back.T
-
-    for i in range(chunks):
-        attend(i)
-        fast_project(head, i)
-        if i >= 1:
-            gathers[i - 1][0].wait_recv()
-            gathers[i - 1][2].start()
-    across = lax.rem(partner + nh // 2, nh)
-    for i in range(chunks - 1):
-        gathers[i][1].wait_recv()
-        fast_project(partner, i)
-        fast_project(peer, i)
-    gathers[chunks - 1][1].wait_recv()
-    fast_project(partner, chunks - 1)
-    for i in range(chunks - 1):
-        gathers[i][2].wait_recv()
-        fast_project(across, i)
-    gathers[chunks - 1][0].wait_recv()
-    gathers[chunks - 1][2].start()
-    fast_project(peer, chunks - 1)
-    gathers[chunks - 1][2].wait_recv()
-    fast_project(across, chunks - 1)
-
-    def compute(part):
-        def body(unit, carry):
-            at = pl.ds(pl.multiple_of(unit * UNIT, UNIT), UNIT)
-            both = dot(s.fk[at], s.guw[part])
+        for part in range(parts):
+            both = dot(key, s.guw[part])
             gate, up = both[:, :LANES], both[:, LANES:]
-            grad = dot(s.og[at], s.dth[:, part * LANES : (part + 1) * LANES])
+            grad = dot(back, s.dth[:, part * LANES : (part + 1) * LANES])
             sig = jax.nn.sigmoid(gate)
             silu = gate * sig
-            s.hk[at] = (silu * up).astype(BF)
-            s.two[at, :LANES] = (grad * up * sig * (1.0 + gate * (1.0 - sig))).astype(BF)
-            s.two[at, LANES:] = (grad * silu).astype(BF)
-            return carry
-
-        lax.fori_loop(0, tokens // UNIT, body, 0, unroll=2)
-        one = dot(s.fkt[...], s.two[...])
-        other = dot(s.ogt[...], s.hk[...])
+            s.hk[part, at] = (silu * up).astype(BF)
+            s.two[part, at, :LANES] = (grad * up * sig * (1.0 + gate * (1.0 - sig))).astype(BF)
+            s.two[part, at, LANES:] = (grad * silu).astype(BF)
+
+    def own_chunk(i, carry):
+        attend(i)
+        copies = emb_copies(i)
+        copies.peer.start()
+        copies.partner.start()
+        fast_project(head, i)
+
+        @pl.when(i >= 1)
+        def _():
+            before = emb_copies(i - 1)
+            before.peer.wait_recv()
+            before.across.start()
+
+        return carry
+
+    lax.fori_loop(0, chunks, own_chunk, 0)
+    across = lax.rem(partner + nh // 2, nh)
+
+    def other_chunk(step, carry):
+        i, which = lax.div(step, 3), lax.rem(step, 3)
+        copies = emb_copies(i)
+
+        @pl.when(which == 0)
+        def _():
+            copies.partner.wait_recv()
+
+        @pl.when(jnp.logical_and(which == 1, i == chunks - 1))
+        def _():
+            copies.peer.wait_recv()
+            copies.across.start()
+
+        @pl.when(which == 2)
+        def _():
+            copies.across.wait_recv()
+
+        fast_project(jnp.where(which == 0, partner, jnp.where(which == 1, peer, across)), i)
+        return carry
+
+    lax.fori_loop(0, 3 * chunks, other_chunk, 0)
+
+    def compute(part):
+        one = dot(s.fkt[...], s.two[part])
+        other = dot(s.ogt[...], s.hk[part])
         s.g[0:width] = one[:width, :LANES]
         s.g[width : 2 * width] = one[:width, LANES:]
         s.g[2 * width : 3 * width] = other[:width]
@@ -551,8 +562,12 @@
 
     for copy in meta_copies + to_peer + to_partner + passed:
         copy.wait_send()
-    for group in x_copies + swaps + gathers:
+    for group in x_copies + swaps:
         for copy in group:
+            copy.wait_send()
+    for i in range(chunks):
+        copies = emb_copies(i)
+        for copy in (copies.peer, copies.partner, copies.across):
             copy.wait_send()
 
 

time: 106 us -> 105 us (level)
  no operation moved by 1% of the time
where the time goes in v4:
time: 105 us
  Pallas kernels  103 us (98%)
  local copies, waits for them, and re-layouts  2.19 us (2%)
    pallas_call x1, Pallas kernels, on_device(): pl.pallas_call(functools.partial(whole_kernel, n, nh, tuple(sizes)), out_...  103 us
    pallas_call x1, local copies, waits for them, and re-layouts, on_device(): pl.pallas_call(functools.partial(whole_kernel, n, nh, tuple(sizes)), out_...  2.19 us

profile of v4, /device:TPU:0, one launch (start us, length us, event | category | flops | bytes accessed | tf_op | source)
XLA Modules:
  0.0 105.1 jit_solution(9611472454121599748)
XLA Ops:
  0.0 102.9 %encode_and_update.1 = bf16[2048,192]{1,0:T(8,128)(2,1)} custom-call(s32[16]{0:T(128)} %dest_ref.1, s32[16]{0:T(128)} %image_ref.1, bf16[16,2,4,32,768]{4,3,2,1,0:T(8,128)(2,1)} %bitcast.10, bf16[3,192,768]{2,1,0:T(8,128)(2,1)} %bitcast.11, bf16[192,768]{1,0:T(8,128)(2,1)} %wo_ref.1, f32[6,128]{1,0:T(8,128)} %bitcast.15, f32[6,128]{1,0:T(8,128)} %bitcast.16, ...), custom_call_target="tpu_custom_call" | custom-call | tf_op jit(solution)/shard_map/encode_and_update/pallas_call | solution.py:594
  102.9 2.2 %copy.12 = bf16[2048,192]{0,1:T(8,128)(2,1)} copy(bf16[2048,192]{1,0:T(8,128)(2,1)} %encode_and_update.1) | data formatting | bytes 1572864 | tf_op jit(solution)/shard_map/encode_and_update/pallas_call | solution.py:594

commit v5 on v4

--- a/solution.py
+++ b/solution.py
@@ -467,45 +467,56 @@
             s.two[part, at, :LANES] = (grad * up * sig * (1.0 + gate * (1.0 - sig))).astype(BF)
             s.two[part, at, LANES:] = (grad * silu).astype(BF)
 
+    across = lax.rem(partner + nh // 2, nh)
+
+    def take_partner(i):
+        emb_copies(i).partner.wait_recv()
+
+    def take_peer(i):
+        copies = emb_copies(i)
+        copies.peer.wait_recv()
+        copies.across.start()
+
     def own_chunk(i, carry):
         attend(i)
         copies = emb_copies(i)
         copies.peer.start()
         copies.partner.start()
-        fast_project(head, i)
-
-        @pl.when(i >= 1)
-        def _():
-            before = emb_copies(i - 1)
-            before.peer.wait_recv()
-            before.across.start()
-
-        return carry
+
+        def one(which, inside):
+            at = i - which
+
+            @pl.when(at >= 0)
+            def _():
+                @pl.when(which == 1)
+                def _():
+                    take_partner(at)
+
+                @pl.when(which == 2)
+                def _():
+                    take_peer(at)
+
+                owner = jnp.where(which == 0, head, jnp.where(which == 1, partner, peer))
+                fast_project(owner, at)
+
+            return inside
+
+        return lax.fori_loop(0, 3, one, carry)
 
     lax.fori_loop(0, chunks, own_chunk, 0)
-    across = lax.rem(partner + nh // 2, nh)
-
-    def other_chunk(step, carry):
-        i, which = lax.div(step, 3), lax.rem(step, 3)
-        copies = emb_copies(i)
-
-        @pl.when(which == 0)
-        def _():
-            copies.partner.wait_recv()
-
-        @pl.when(jnp.logical_and(which == 1, i == chunks - 1))
-        def _():
-            copies.peer.wait_recv()
-            copies.across.start()
-
-        @pl.when(which == 2)
-        def _():
-            copies.across.wait_recv()
-
-        fast_project(jnp.where(which == 0, partner, jnp.where(which == 1, peer, across)), i)
-        return carry
-
-    lax.fori_loop(0, 3 * chunks, other_chunk, 0)
+    take_partner(chunks - 1)
+    fast_project(partner, chunks - 1)
+    emb_copies(0).across.wait_recv()
+    fast_project(across, 0)
+    take_peer(chunks - 2)
+    fast_project(peer, chunks - 2)
+    for i in range(1, chunks - 1):
+        emb_copies(i).across.wait_recv()
+        fast_project(across, i)
+    take_peer(chunks - 1)
+    fast_project(peer, chunks - 1)
+    emb_copies(chunks - 1).across.wait_recv()
+    fast_project(across, chunks - 1)
 
     def compute(part):
         one = dot(s.fkt[...], s.two[part])

time: 105 us -> 100 us (0.952)
  Pallas kernels: 103 us -> 97.9 us
    pallas_call x1, Pallas kernels: 103 us -> 97.9 us  [on_device(): pl.pallas_call(functools.partial(whole_kernel, n, nh, tuple(sizes)), out_...]
where the time goes in v5:
time: 100 us
  Pallas kernels  97.9 us (98%)
  local copies, waits for them, and re-layouts  2.19 us (2%)
    pallas_call x1, Pallas kernels, on_device(): pl.pallas_call(functools.partial(whole_kernel, n, nh, tuple(sizes)), out_...  97.9 us
    pallas_call x1, local copies, waits for them, and re-layouts, on_device(): pl.pallas_call(functools.partial(whole_kernel, n, nh, tuple(sizes)), out_...  2.19 us

profile of v5, /device:TPU:0, one launch (start us, length us, event | category | flops | bytes accessed | tf_op | source)
XLA Modules:
  0.0 100.1 jit_solution(10170358092652587764)
XLA Ops:
  0.0 97.9 %encode_and_update.1 = bf16[2048,192]{1,0:T(8,128)(2,1)} custom-call(s32[16]{0:T(128)} %dest_ref.1, s32[16]{0:T(128)} %image_ref.1, bf16[16,2,4,32,768]{4,3,2,1,0:T(8,128)(2,1)} %bitcast.10, bf16[3,192,768]{2,1,0:T(8,128)(2,1)} %bitcast.11, bf16[192,768]{1,0:T(8,128)(2,1)} %wo_ref.1, f32[6,128]{1,0:T(8,128)} %bitcast.15, f32[6,128]{1,0:T(8,128)} %bitcast.16, ...), custom_call_target="tpu_custom_call" | custom-call | tf_op jit(solution)/shard_map/encode_and_update/pallas_call | solution.py:605
  97.9 2.2 %copy.12 = bf16[2048,192]{0,1:T(8,128)(2,1)} copy(bf16[2048,192]{1,0:T(8,128)(2,1)} %encode_and_update.1) | data formatting | bytes 1572864 | tf_op jit(solution)/shard_map/encode_and_update/pallas_call | solution.py:605

commit v6 on v5

--- a/solution.py
+++ b/solution.py
@@ -166,15 +166,16 @@
             plans[part].r[t - 1].wait_recv()
             plans[part].f[t - 1].start()
 
-    stages = [stage_x, stage_z, stage_r, stage_f]
-    for tick in range(parts + len(stages) - 1):
-        if tick < parts:
-            compute(tick)
-        for which, stage in enumerate(stages):
-            if 0 <= tick - which < parts:
-                stage(tick - which)
-        if tick == parts - 1:
-            during()
+    for part in range(parts):
+        compute(part)
+        stage_x(part)
+    for part in range(parts):
+        stage_z(part)
+    during()
+    for part in range(parts):
+        stage_r(part)
+    for part in range(parts):
+        stage_f(part)
     for part in range(parts):
         plans[part].r[-1].wait_recv()
         for copy in plans[part].f:
@@ -298,7 +299,8 @@
     ]
     pick(0)
     pl.semaphore_wait(barrier, len(greeted))
-    for copy in meta_copies + x_copies[0]:
+    far_first = sorted(range(n - 1), key=lambda step: abs(step + 1 - n // 2))
+    for copy in meta_copies + [x_copies[0][step] for step in far_first]:
         copy.start()
     for copy in weights_in:
         copy.wait()
@@ -306,8 +308,8 @@
         copy.start()
     for c in range(1, STEPS):
         pick(c)
-        for copy in x_copies[c]:
-            copy.start()
+        for step in far_first:
+            x_copies[c][step].start()
 
     s.wf[...] = jnp.zeros_like(s.wf)
     s.v[...] = jnp.ones_like(s.v)

time: 100 us -> 97.6 us (0.976)
  Pallas kernels: 97.9 us -> 95.2 us
    pallas_call x1, Pallas kernels: 97.9 us -> 95.2 us  [on_device(): pl.pallas_call(functools.partial(whole_kernel, n, nh, tuple(sizes)), out_...]
where the time goes in v6:
time: 97.6 us; the launch traced here: 97.4 us
  Pallas kernels  95.2 us (98%)
  local copies, waits for them, and re-layouts  2.19 us (2%)
    pallas_call x1, Pallas kernels, on_device(): pl.pallas_call(functools.partial(whole_kernel, n, nh, tuple(sizes)), out_...  95.2 us
    pallas_call x1, local copies, waits for them, and re-layouts, on_device(): pl.pallas_call(functools.partial(whole_kernel, n, nh, tuple(sizes)), out_...  2.19 us

profile of v6, /device:TPU:0, one launch (start us, length us, event | category | flops | bytes accessed | tf_op | source)
XLA Modules:
  0.0 97.4 jit_solution(833860921011770872)
XLA Ops:
  0.0 95.2 %encode_and_update.1 = bf16[2048,192]{1,0:T(8,128)(2,1)} custom-call(s32[16]{0:T(128)} %dest_ref.1, s32[16]{0:T(128)} %image_ref.1, bf16[16,2,4,32,768]{4,3,2,1,0:T(8,128)(2,1)} %bitcast.10, bf16[3,192,768]{2,1,0:T(8,128)(2,1)} %bitcast.11, bf16[192,768]{1,0:T(8,128)(2,1)} %wo_ref.1, f32[6,128]{1,0:T(8,128)} %bitcast.15, f32[6,128]{1,0:T(8,128)} %bitcast.16, ...), custom_call_target="tpu_custom_call" | custom-call | tf_op jit(solution)/shard_map/encode_and_update/pallas_call | solution.py:607
  95.2 2.2 %copy.12 = bf16[2048,192]{0,1:T(8,128)(2,1)} copy(bf16[2048,192]{1,0:T(8,128)(2,1)} %encode_and_update.1) | data formatting | bytes 1572864 | tf_op jit(solution)/shard_map/encode_and_update/pallas_call | solution.py:607

commit v7 on v6

--- a/solution.py
+++ b/solution.py
@@ -15,7 +15,7 @@
 EPSILON = 1e-06
 RATE_SCALE = 0.1
 LANES = 128
-STEPS = 4
+STEPS = 8
 CHUNK = 128
 UNIT = 256
 MESH = pl.DeviceIdType.MESH

time: 97.6 us -> 105 us (1.076)
  Pallas kernels: 95.2 us -> 103 us
    pallas_call x1, Pallas kernels: 95.2 us -> 103 us  [on_device(): pl.pallas_call(functools.partial(whole_kernel, n, nh, tuple(sizes)), out_...]
where the time goes in v7:
time: 105 us
  Pallas kernels  103 us (98%)
  local copies, waits for them, and re-layouts  2.19 us (2%)
    pallas_call x1, Pallas kernels, on_device(): pl.pallas_call(functools.partial(whole_kernel, n, nh, tuple(sizes)), out_...  103 us
    pallas_call x1, local copies, waits for them, and re-layouts, on_device(): pl.pallas_call(functools.partial(whole_kernel, n, nh, tuple(sizes)), out_...  2.19 us

profile of v7, /device:TPU:0, one launch (start us, length us, event | category | flops | bytes accessed | tf_op | source)
XLA Modules:
  0.0 105.3 jit_solution(15434496931678530161)
XLA Ops:
  0.0 103.1 %encode_and_update.1 = bf16[2048,192]{1,0:T(8,128)(2,1)} custom-call(s32[16]{0:T(128)} %dest_ref.1, s32[16]{0:T(128)} %image_ref.1, bf16[16,2,8,16,768]{4,3,2,1,0:T(8,128)(2,1)} %bitcast.10, bf16[3,192,768]{2,1,0:T(8,128)(2,1)} %bitcast.11, bf16[192,768]{1,0:T(8,128)(2,1)} %wo_ref.1, f32[6,128]{1,0:T(8,128)} %bitcast.15, f32[6,128]{1,0:T(8,128)} %bitcast.16, ...), custom_call_target="tpu_custom_call" | custom-call | tf_op jit(solution)/shard_map/encode_and_update/pallas_call | solution.py:607
  103.1 2.2 %copy.12 = bf16[2048,192]{0,1:T(8,128)(2,1)} copy(bf16[2048,192]{1,0:T(8,128)(2,1)} %encode_and_update.1) | data formatting | bytes 1572864 | tf_op jit(solution)/shard_map/encode_and_update/pallas_call | solution.py:607
